TPU v7x, 256 devices: a whole 4x4x8 slice. The times are simulated.
256 devices in a mesh: dp: 4 (over x), vocab: 64 (over z, y, core).
Axes of the slice: x: 4, y: 4, z: 8, core: 2. Of those that a mesh axis runs over, the one named last changes fastest.
Arguments:
- prefill_hidden: bfloat16 [1024, 7168], P(('dp', 'vocab')), may hold values from -60 to 60
- decode_hidden: bfloat16 [256, 7168], P(('dp', 'vocab')), may hold values from -60 to 60
- lm_head: bfloat16 [7168, 129280], P('dp', 'vocab'), as said below
- prefill_targets: int32 [1024], P(('dp', 'vocab')), may hold values from 0 to 129279
- decode_targets: int32 [256], P(('dp', 'vocab')), may hold values from 0 to 129279
- decode_live: int32 [4], P('dp'), may hold values from 1 to 64
Outputs:
- prefill_logprob: float32 [1024], P(('dp', 'vocab'))
- decode_logprob: float32 [256], P(('dp', 'vocab'))
Inputs may be any that keep to these rules, and one draw needn't show every extreme that they name: `lm_head`: entries of order one over the square root of 7168.
All inputs are finite; a program needn't handle non-finite values.
Results may differ from a plain program's by a relative error of at most 0.0003.
Values may be sent and summed in bfloat16 or wider, within the bound.
A program may use at most 128 MiB of HBM per device.

v0:
```python
import jax
import jax.numpy as jnp
from jax import lax
from jax.sharding import Mesh
from jax.sharding import PartitionSpec as P

VOCAB = ("vocab_0", "vocab_1", "vocab_2")
DP_VOCAB = ("dp", "vocab_0", "vocab_1", "vocab_2")


def gathered_once(value, axis):
    leaves = jax.tree.leaves(value)
    sequence = sorted(range(len(leaves)), key=lambda k: -leaves[k].size)
    width = (1, *leaves[sequence[0]].shape)[-1]
    lines = [
        jnp.pad(leaves[k].reshape(-1), (0, -leaves[k].size % width)).reshape(-1, width)
        for k in sequence
    ]
    both, at, found = (lax.all_gather(jnp.concatenate(lines), axis), 0, {})
    for k, line in zip(sequence, lines):
        slab = both[:, at : at + len(line)].reshape(len(both), -1)
        found[k] = slab[:, : leaves[k].size].reshape(-1, *leaves[k].shape)
        at += len(line)
    numbers = iter(range(len(leaves)))
    return jax.tree.map(lambda _: found[next(numbers)], value)


def joined_all(value, axes, combine):
    for axis in axes:
        pieces = gathered_once(value, axis)
        value = jax.tree.map(lambda part: part[0], pieces)
        for k in range(1, lax.axis_size(axis)):
            value = combine(value, jax.tree.map(lambda part: part[k], pieces))
    return value


def softmax_join(left, right):
    new_top = jnp.maximum(left[0], right[0])
    totals = left[1] * jnp.exp(left[0] - new_top) + right[1] * jnp.exp(right[0] - new_top)
    return (new_top, totals, left[2] + right[2])


def body(prefill_hidden, decode_hidden, lm_head, prefill_targets, decode_targets, decode_live):
    pre_rows = prefill_hidden.shape[0]
    dec_rows = decode_hidden.shape[0]
    own_count = pre_rows + dec_rows
    hidden = jnp.concatenate([prefill_hidden, decode_hidden], axis=0)
    targets = jnp.concatenate([prefill_targets, decode_targets], axis=0)
    shard_vocab = lm_head.shape[1]
    vocab_offset = lax.axis_index(VOCAB) * shard_vocab
    group_hidden, group_targets = (
        lax.all_gather(hidden, VOCAB, axis=0, tiled=True),
        lax.all_gather(targets, VOCAB, axis=0, tiled=True),
    )
    every_rows = lax.all_to_all(group_hidden, "dp", split_axis=1, concat_axis=0, tiled=True)
    logits = lax.psum_scatter(
        jnp.dot(every_rows, lm_head, preferred_element_type=jnp.float32),
        "dp",
        scatter_dimension=0,
        tiled=True,
    )
    local_top = jnp.max(logits, axis=1)
    target_hit = (group_targets - vocab_offset)[:, None] == jnp.arange(
        shard_vocab, dtype=jnp.int32
    )[None, :]
    local_picked = jnp.sum(jnp.where(target_hit, logits, jnp.float32(0.0)), axis=1)
    own_start = lax.axis_index(VOCAB) * own_count
    local_total = jnp.sum(jnp.exp(logits - local_top[:, None]), axis=1)
    row_top, totals, picked = joined_all(
        (local_top, local_total, local_picked), VOCAB, softmax_join
    )
    group_values = picked - (row_top + jnp.log(totals))
    own_values = lax.dynamic_slice_in_dim(group_values, own_start, own_count, 0)
    prefill_logprob = own_values[:pre_rows]
    positions = lax.axis_index(VOCAB) * dec_rows + jnp.arange(dec_rows, dtype=jnp.int32)
    decode_logprob = jnp.where(positions < decode_live[0], own_values[pre_rows:], jnp.float32(0.0))
    return (prefill_logprob, decode_logprob)


def solution(mesh):
    split = Mesh(
        mesh.devices.reshape(mesh.shape["dp"], 8, 4, 2), ("dp", "vocab_0", "vocab_1", "vocab_2")
    )
    placed = (
        P(DP_VOCAB, None),
        P(DP_VOCAB, None),
        P("dp", VOCAB),
        P(DP_VOCAB),
        P(DP_VOCAB),
        P("dp"),
    )
    return jax.shard_map(
        body, mesh=split, in_specs=placed, out_specs=(P(DP_VOCAB), P(DP_VOCAB)), check_vma=False
    )
```

profile of v0, /device:TPU:5, one launch (start us, length us, event | category | flops | bytes accessed | tf_op | source)
XLA Modules:
  0.0 328.5 jit_solution(16008943737655418088)
XLA Ops:
  7.2 0.0 all-gather.9.cloned.1.call-start
  7.2 1.5 maximum_bitcast_fusion
  8.8 0.0 all-gather.9.cloned.1.call-update
  8.8 0.0 reduce-scatter.2.cloned.1.call-start
  8.8 87.0 %all-gather.9.cloned.1.call-done = bf16[64,5,7168]{2,1,0:T(8,128)(2,1)} async-done(((bf16[1,5,7168]{2,1,0:T(8,128)(2,1)}), bf16[64,5,7168]{2,1,0:T(8,128)(2,1)}) %all-gather.9.cloned.1.call-update) | async-done | bytes 4587536 | tf_op jit(solution)/shard_map/all_gather | solution.py:52
  95.8 11.4 %all_to_all.14 = bf16[320,4,1792]{2,1,0:T(4,128)(2,1)} reshape(bf16[64,5,7168]{2,1,0:T(8,128)(2,1)} %all-gather.9.cloned.1.call-done) | data formatting | bytes 9175040 | tf_op jit(solution)/shard_map/all_to_all | solution.py:55
  107.3 0.0 slice-start
  107.3 3.0 copy.9
  110.3 0.0 slice-start.1
  110.3 54.2 %all_to_all.19 = bf16[320,4,1792]{2,0,1:T(8,128)(2,1)S(1)} all-to-all(bf16[320,4,1792]{2,0,1:T(8,128)(2,1)S(1)} %copy.9), channel_id=1, replica_groups=mesh['dp'=4,'vocab_0'=8,'vocab_1'=4,'vocab_2'=2] {'dp'}, dimensions={1} | all-to-all | bytes 9175040 | tf_op jit(solution)/shard_map/all_to_all | solution.py:55
  164.5 0.0 slice-done
  164.5 0.0 slice-done.1
  164.5 12.4 %fusion.47 = f32[1280,2020]{1,0:T(8,128)} fusion(bf16[1280,1792]{1,0:T(8,128)(2,1)S(1)} %bitcast.248, bf16[1792,2020]{0,1:T(8,128)(2,1)S(1)} %bitcast.250), kind=kOutput, calls=%fused_computation.95 | convolution fusion | flops 9266790400 | bytes 22169600 | tf_op jit(solution)/shard_map/dot_general | solution.py:57
  176.9 0.0 copy-start.1
  176.9 0.0 copy-start
  176.9 0.0 reduce-scatter.2.cloned.1.call-update
  178.2 0.0 copy-done.1
  178.3 0.6 dynamic-slice
  179.5 0.0 copy-done
  179.5 0.2 add_dynamic-update-slice_fusion
  179.7 14.9 %all-reduce = s32[320]{0:T(512)S(1)} all-reduce(s32[320]{0:T(512)S(1)} %add_dynamic-update-slice_fusion), channel_id=1, replica_groups=mesh['dp'=4,'vocab_0'=8,'vocab_1'=4,'vocab_2'=2] {'vocab_0','vocab_1','v..., use_global_device_ids=true, to_apply=%add | all-reduce | flops 320 | bytes 2560
  194.6 79.1 %reduce-scatter.2.cloned.1.call-done = f32[320,2020]{1,0:T(8,128)} async-done(((f32[1280,2020]{1,0:T(8,128)}), f32[320,2020]{1,0:T(8,128)}) %reduce-scatter.2.cloned.1.call-update) | async-done | bytes 2585616 | tf_op jit(solution)/shard_map/reduce_scatter | solution.py:56
  273.7 2.0 reduce_max.9
  275.6 2.5 exponential_reduce_fusion
  278.2 20.2 %all-gather.4 = f32[8,3,320]{2,1,0:T(4,128)S(1)} all-gather(f32[1,3,320]{2,1,0:T(4,128)S(1)} %maximum_bitcast_fusion.1), channel_id=2, replica_groups=mesh['dp'=4,'vocab_0'=8,'vocab_1'=4,'vocab_2'=2] {'vocab_0'}, dimensions={0}, use_global_device_ids=true | all-gather | bytes 34560 | tf_op jit(solution)/shard_map/all_gather | solution.py:19
  298.5 9.4 %all-gather.5 = f32[4,3,320]{2,1,0:T(4,128)S(1)} all-gather(f32[1,3,320]{2,1,0:T(4,128)S(1)} %maximum_bitcast_fusion.2), channel_id=3, replica_groups=mesh['dp'=4,'vocab_0'=8,'vocab_1'=4,'vocab_2'=2] {'vocab_1'}, dimensions={0}, use_global_device_ids=true | all-gather | bytes 19200 | tf_op jit(solution)/shard_map/all_gather | solution.py:19
  308.0 11.1 %all-gather.6 = f32[2,3,320]{2,1,0:T(4,128)S(1)} all-gather(f32[1,3,320]{2,1,0:T(4,128)S(1)} %maximum_bitcast_fusion.3), channel_id=4, replica_groups=mesh['dp'=4,'vocab_0'=8,'vocab_1'=4,'vocab_2'=2] {'vocab_2'}, dimensions={0}, use_global_device_ids=true | all-gather | bytes 11520 | tf_op jit(solution)/shard_map/all_gather | solution.py:19
  319.2 0.1 dynamic_slice.3
  319.3 0.0 copy-start.2
  319.3 0.6 slice.268
  320.5 0.0 copy-done.2
  (15 shorter events, 0.2 us)
Async XLA Ops:
  7.2 88.7 %all-gather.9.cloned.1.call-start = ((), (), s32[]{:S(2)}) async-start(), calls=%async_computation.3 | async-start | bytes 7454720 | tf_op jit(solution)/shard_map/all_gather | solution.py:52
  8.8 264.9 %reduce-scatter.2.cloned.1.call-start = ((), (), s32[]{:S(2)}) async-start(), calls=%async_computation.2 | async-start | bytes 13107200 | tf_op jit(solution)/shard_map/reduce_scatter | solution.py:56
  107.3 57.2 %slice-start = ((s8[7254016]{0:T(1024)(128)(4,1)}), s8[4194304]{0:T(1024)(128)(4,1)S(1)}, s32[]{:S(2)}) async-start(s8[7254016]{0:T(1024)(128)(4,1)} %bitcast.249), calls=%async_computation.4 | async-start | bytes 8388608
  110.3 54.2 %slice-start.1 = ((s8[7254016]{0:T(1024)(128)(4,1)}), s8[3059712]{0:T(1024)(128)(4,1)S(1)}, s32[]{:S(2)}) async-start(s8[7254016]{0:T(1024)(128)(4,1)} %bitcast.249), calls=%async_computation.5 | async-start | bytes 6119424
  176.9 1.3 copy-start.1
  176.9 2.6 copy-start
  319.3 1.2 copy-start.2
Sparse Core Ops, SparseCore 0:
  10.7 85.0 all-gather.8
  177.1 96.5 reduce-scatter.1
where the time goes:
time: 331 us; the launch traced here: 328 us
  waiting for transfers between devices  166 us (50%)
  blocking collectives  110 us (33%)
  between operations  17.9 us (5%)
  local copies, waits for them, and re-layouts  15.7 us (5%)
  matrix products  12.4 us (4%)
  other arithmetic  6.4 us (2%)
    all_gather x1, waiting for transfers between devices, body(): lax.all_gather(hidden, VOCAB, axis=0, tiled=True)  87 us
    reduce_scatter x1, waiting for transfers between devices, body(): lax.psum_scatter(jnp.dot(every_rows, lm_head, preferred_element_type=jnp....  79.1 us
    all_to_all x1, blocking collectives, body(): lax.all_to_all(group_hidden, 'dp', split_axis=1, concat_axis=0, tiled=True)  54.2 us
    all_gather x3, blocking collectives, gathered_once(): both, at, found = (lax.all_gather(jnp.concatenate(lines), axis), 0, {})  40.8 us
    unnamed x1, blocking collectives  14.9 us
    all_to_all x2, local copies, waits for them, and re-layouts, body(): lax.all_to_all(group_hidden, 'dp', split_axis=1, concat_axis=0, tiled=True)  14.5 us
    dot_general x1, matrix products, body(): jnp.dot(every_rows, lm_head, preferred_element_type=jnp.float32)  12.4 us
  transfers between devices with their start and end apart: 2, of which 2 were waited for; matrix products, arithmetic and copies ran while one was open for 0% of the time, Pallas kernels for 0%

commit v1 on v0

v1 whole, which is shorter than its diff:
```python
import jax
import jax.numpy as jnp
from jax import lax
from jax.experimental import pallas as pl
from jax.experimental.pallas import tpu as pltpu
from jax.sharding import Mesh
from jax.sharding import PartitionSpec as P

VOCAB = ("z", "y", "c")
DP_VOCAB = ("dp", "z", "y", "c")
MESH = pl.DeviceIdType.MESH
GROUP = 16
TOP = 32000.0
STAT = 256


def make_kernel(nx, nz, ny, nc, rows, depth, vocab):
    pieces_n = nx * nc
    small = pieces_n * rows
    block = ny * small
    half = block // 2
    padded = -(-vocab // 512) * 512
    last = padded - 128
    nb = nz // nx

    def kernel(pre_ref, dec_ref, pt_ref, dt_ref, w_hbm, out_ref,
               w, pieces, xrecv, f40, ybuf, fblk, hall, part, sbuf, relay, rdst,
               stat, tt, st, cst, yst, zst, res,
               w_sem, xs, xr, ys, yr, ags, agr, d2s, d2r, ts, tr, rs, rlr, rdr,
               cs, cr, y2s, y2r, z2s, z2r, x2s, x2r):
        x = lax.axis_index("dp")
        z = lax.axis_index("z")
        y = lax.axis_index("y")
        c = lax.axis_index("c")
        other = 1 - c
        me = x * nc + c
        w_copy = pltpu.make_async_copy(w_hbm, w, w_sem)
        w_copy.start()

        def send(src, dst, ssem, rsem, dev):
            return pltpu.make_async_remote_copy(
                src_ref=src, dst_ref=dst, send_sem=ssem, recv_sem=rsem,
                device_id=dev, device_id_type=MESH)

        def arrival(dst, sem):
            return send(dst, dst, sem, sem, (x, z, y, other))

        barrier = pltpu.get_barrier_semaphore()
        peers = []
        for k in range(1, pieces_n):
            p = lax.rem(me + k, pieces_n)
            peers.append((lax.div(p, nc), z, y, lax.rem(p, nc)))
        for k in range(1, ny):
            peers.append((x, z, lax.rem(y + k, ny), c))
        for k in range(1, nz):
            peers.append((x, lax.rem(z + k, nz), y, c))
        for dev in peers:
            pl.semaphore_signal(barrier, inc=1, device_id=dev, device_id_type=MESH)

        n_pre = pre_ref.shape[0]
        n_dec = dec_ref.shape[0]
        for p in range(pieces_n):
            cols = slice(p * depth, (p + 1) * depth)
            pieces[p, 0:n_pre, 0:depth] = pre_ref[:, cols].astype(jnp.float32)
            pieces[p, n_pre:rows, 0:depth] = dec_ref[:, cols].astype(jnp.float32)
        for r in range(rows):
            t = pt_ref[r] if r < n_pre else dt_ref[r - n_pre]
            tv = jnp.full((1, 128), t, jnp.int32).astype(jnp.float32)
            for p in range(pieces_n):
                pieces[p, r:r + 1, depth:depth + 128] = tv
        for p in range(pieces_n):
            pieces[p, rows:8, :] = jnp.zeros((8 - rows, depth + 128), jnp.float32)
        for k in range(nz):
            for h in range(2):
                part[k, h, :, last:padded] = jnp.zeros((half, 128), jnp.float32)
        stat[...] = jnp.zeros(stat.shape, jnp.float32)

        pl.semaphore_wait(barrier, len(peers))

        def x_copy(k):
            p = lax.rem(me + k, pieces_n)
            return send(pieces.at[p], xrecv.at[me], xs.at[p], xr.at[me],
                        (lax.div(p, nc), z, y, lax.rem(p, nc)))

        for k in range(1, pieces_n):
            x_copy(k).start()
        xrecv[me] = pieces[me]
        for k in range(1, pieces_n):
            p = lax.rem(me + k, pieces_n)
            arrival(xrecv.at[p], xr.at[p]).wait_recv()
        for s in range(pieces_n):
            f40[s * rows:(s + 1) * rows, :] = xrecv[s, 0:rows, :]

        lane = lax.broadcasted_iota(jnp.int32, (small, 128), 1)
        tcol = f40[:, depth:depth + 128]
        t1 = jnp.floor(tcol * (1.0 / 256.0))
        t2 = jnp.floor(t1 * (1.0 / 256.0))
        digits = jnp.where(lane == 0, tcol - 256.0 * t1,
                           jnp.where(lane == 1, t1 - 256.0 * t2,
                                     jnp.where(lane == 2, t2, 0.0)))
        ybuf[y, :, 0:depth] = f40[:, 0:depth].astype(jnp.bfloat16)
        ybuf[y, :, depth:depth + 128] = digits.astype(jnp.bfloat16)

        def y_copy(k):
            yy = lax.rem(y + k, ny)
            return send(ybuf.at[y], ybuf.at[y], ys.at[yy], yr.at[y], (x, z, yy, c))

        for k in range(1, ny):
            y_copy(k).start()
        for k in range(1, ny):
            yy = lax.rem(y + k, ny)
            arrival(ybuf.at[yy], yr.at[yy]).wait_recv()
        for s in range(ny):
            fblk[s * small:(s + 1) * small, :] = ybuf[s].astype(jnp.float32)
        hall[c, z] = fblk[:, 0:depth].astype(jnp.bfloat16)

        def own_copy(way):
            zz = lax.rem(z + (1 if way else nz - 1), nz)
            return send(hall.at[c, z], hall.at[c, z], ags.at[nz if way else z], agr.at[z],
                        (x, zz, y, c))

        def core_copy(zb):
            return send(hall.at[c, zb], hall.at[c, zb], d2s.at[zb], d2r.at[zb], (x, z, y, other))

        own_copy(0).start()
        own_copy(1).start()
        core_copy(z).start()

        slot = lax.div(z, nx)
        reducer = lax.rem(z, nx) == x
        digit = lax.broadcasted_iota(jnp.int32, (block, 128), 1)
        weight = jnp.where(digit == 0, 1.0, jnp.where(digit == 1, 256.0,
                                                      jnp.where(digit == 2, 65536.0, 0.0)))
        ids = jnp.sum(fblk[:, depth:depth + 128] * weight, axis=1, keepdims=True)
        stat[0:block, :] = jnp.broadcast_to(ids, (block, 128))

        def tile_of():
            for k in range(STAT // 128):
                yield k, jnp.transpose(stat[k * 128:(k + 1) * 128, :])[0:8, :]

        def t_copy(k):
            zz = lax.rem(z + k, nz)
            return send(tt.at[slot], tt.at[slot], ts.at[zz], tr.at[slot], (x, zz, y, c))

        @pl.when(reducer)
        def _():
            for k, tile in tile_of():
                tt[slot, :, k * 128:(k + 1) * 128] = tile
            for k in range(1, nz):
                t_copy(k).start()

        w_copy.wait()

        def offset(i):
            odd = lax.rem(i, 2)
            dist = lax.div(i + 1, 2)
            zb = lax.rem(z + nz + jnp.where(odd == 1, dist, -dist), nz)
            return odd, dist, zb

        def role_of(zb):
            return lax.rem(x + nx * nz - zb, nx)

        def forward(i):
            odd, dist, zb = offset(i)
            zz = lax.rem(z + jnp.where(odd == 1, nz - 1, 1), nz)
            go = dist < jnp.where(odd == 1, nz // 2, nz - nz // 2 - 1)
            copy = send(hall.at[c, zb], hall.at[c, zb], ags.at[zb], agr.at[zb], (x, zz, y, c))
            return jnp.logical_and(i > 0, go), copy

        def quantise(zb, h, relayed):
            @pl.loop(0, half // GROUP)
            def _(g):
                at = pl.ds(pl.multiple_of(g * GROUP, GROUP), GROUP)
                v = part[zb, h, at, :]
                if relayed:
                    v = v + unpack(relay[zb, at, :])
                big = jnp.max(jnp.abs(v), axis=1, keepdims=True)
                e = jnp.ceil(jnp.log2(jnp.maximum(big, 1e-20) * (1.0 / TOP)))
                q = jnp.round(v * jnp.exp2(-e))
                tail = lax.broadcasted_iota(jnp.int32, q.shape, 1) >= vocab
                q = jnp.where(tail, e, q)
                sbuf[zb, h, at, :] = q.astype(jnp.int32).astype(jnp.int16)

        def unpack(code):
            v = code.astype(jnp.int32).astype(jnp.float32)
            e = v[:, padded - 1:padded]
            tail = lax.broadcasted_iota(jnp.int32, v.shape, 1) >= vocab
            return jnp.where(tail, 0.0, v * jnp.exp2(e))

        def relay_copy(zb, h):
            xx = lax.rem(x + jnp.where(h == 0, nx - 1, 1), nx)
            return send(sbuf.at[zb, h], relay.at[zb], rs.at[zb, h], rlr.at[zb], (xx, z, y, c))

        def final_copy(zb, h, side):
            xx = lax.rem(x + jnp.where(side == 0, nx - 1, 1), nx)
            b = lax.div(zb, nx)
            return send(sbuf.at[zb, h], rdst.at[b, side, h], rs.at[zb, h], rdr.at[b, side, h],
                        (xx, z, y, c))

        def step(i, carry):
            odd, dist, zb = offset(i)

            @pl.when(i > 0)
            def _():
                arrival(hall.at[c, zb], agr.at[zb]).wait_recv()
                core_copy(zb).start()

            go, copy = forward(i)

            @pl.when(go)
            def _():
                copy.start()

            arrival(hall.at[other, zb], d2r.at[zb]).wait_recv()
            for n in range(padded // 512):
                n0, n1 = n * 512, min(n * 512 + 512, vocab)
                acc = jnp.dot(hall[0, zb], w[0:depth, n0:n1], preferred_element_type=jnp.float32)
                acc += jnp.dot(hall[1, zb], w[depth:2 * depth, n0:n1],
                               preferred_element_type=jnp.float32)
                part[zb, 0, :, n0:n1] = acc[0:half]
                part[zb, 1, :, n0:n1] = acc[half:block]
            role = role_of(zb)

            @pl.when(role == 2)
            def _():
                for h in range(2):
                    quantise(zb, h, False)
                    relay_copy(zb, h).start()

            @pl.when(lax.rem(role, 2) == 1)
            def _():
                h = jnp.where(role == 1, 1, 0)
                quantise(zb, h, False)
                final_copy(zb, h, jnp.where(role == 1, 0, 1)).start()

            return carry

        lax.fori_loop(0, nz, step, 0)

        def pass_on(i, carry):
            odd, dist, zb = offset(i)
            role = role_of(zb)

            @pl.when(lax.rem(role, 2) == 1)
            def _():
                h = jnp.where(role == 1, 0, 1)
                arrival(relay.at[zb], rlr.at[zb]).wait_recv()
                quantise(zb, h, True)
                final_copy(zb, h, jnp.where(role == 1, 0, 1)).start()

            return carry

        lax.fori_loop(0, nz, pass_on, 0)

        first = ((z * ny + y) * nc + c) * vocab
        firstf = first.astype(jnp.float32)

        def reduce(b, carry):
            zb = x + nx * b

            @pl.when(zb != z)
            def _():
                arrival(tt.at[b], tr.at[b]).wait_recv()

            for k in range(STAT // 128):
                cols = jnp.broadcast_to(tt[b, 0:1, k * 128:(k + 1) * 128], (128, 128))
                stat[k * 128:(k + 1) * 128, :] = jnp.transpose(cols)
            for h in range(2):
                for side in range(2):
                    arrival(rdst.at[b, side, h], rdr.at[b, side, h]).wait_recv()

                @pl.loop(0, half // GROUP)
                def _(g):
                    at = pl.ds(pl.multiple_of(g * GROUP, GROUP), GROUP)
                    rat = pl.ds(pl.multiple_of(h * half + g * GROUP, GROUP), GROUP)
                    v = part[zb, h, at, :] + (unpack(rdst[b, 0, h, at, :])
                                              + unpack(rdst[b, 1, h, at, :]))
                    col = lax.broadcasted_iota(jnp.int32, v.shape, 1)
                    local = (stat[rat, 0:1] - firstf).astype(jnp.int32)
                    picked = jnp.sum(jnp.where(col == local, v, 0.0), axis=1, keepdims=True)
                    v = jnp.where(col >= vocab, -jnp.inf, v)
                    top = jnp.max(v, axis=1, keepdims=True)
                    total = jnp.sum(jnp.exp(v - top), axis=1, keepdims=True)
                    ln = lax.broadcasted_iota(jnp.int32, (GROUP, 128), 1)
                    picked = jnp.where(jnp.logical_and(local >= 0, local < vocab), picked, 0.0)
                    stat[rat, :] = jnp.where(ln == 0, top, jnp.where(ln == 1, total,
                                                                    jnp.where(ln == 2, picked, 0.0)))
            for k, tile in tile_of():
                st[b, :, k * 128:(k + 1) * 128] = tile
            return carry

        lax.fori_loop(0, nb, reduce, 0)

        def join(tiles):
            tops = [t[0:1, :] for t in tiles]
            top = tops[0]
            for t in tops[1:]:
                top = jnp.maximum(top, t)
            total, picked = 0.0, 0.0
            for t, m in zip(tiles, tops):
                total += t[1:2, :] * jnp.exp(m - top)
                picked += t[2:3, :]
            return top, total, picked

        def put(ref, joined):
            top, total, picked = joined
            row = lax.broadcasted_iota(jnp.int32, (8, STAT), 0)
            ref[...] = jnp.where(row == 0, top, jnp.where(row == 1, total,
                                                          jnp.where(row == 2, picked, 0.0)))

        c_copy = send(st.at[other], cst, cs, cr, (x, z, y, other))
        c_copy.start()
        arrival(cst, cr).wait_recv()
        put(yst.at[y], join([st[c], cst[...]]))

        def y2_copy(k):
            yy = lax.rem(y + k, ny)
            return send(yst.at[y], yst.at[y], y2s.at[yy], y2r.at[y], (x, z, yy, c))

        for k in range(1, ny):
            y2_copy(k).start()
        for k in range(1, ny):
            yy = lax.rem(y + k, ny)
            arrival(yst.at[yy], y2r.at[yy]).wait_recv()
        put(zst.at[z], join([yst[k] for k in range(ny)]))
        home = x + nx * c
        z2_copy = send(zst.at[z], zst.at[z], z2s, z2r.at[z], (x, home, y, c))

        @pl.when(z != home)
        def _():
            z2_copy.start()

        def x2_copy(k):
            p = lax.rem(me + k, pieces_n)
            return send(res, out_ref, x2s.at[p], x2r, (lax.div(p, nc), z, y, lax.rem(p, nc)))

        @pl.when(z == home)
        def _():
            for k in range(1, nz):
                zz = lax.rem(z + k, nz)
                arrival(zst.at[zz], z2r.at[zz]).wait_recv()
            top, total, picked = join([zst[k] for k in range(nz)])
            value = jnp.broadcast_to(picked - (top + jnp.log(total)), (8, STAT))
            res[...] = value
            for k in range(1, pieces_n):
                x2_copy(k).start()
            out_ref[...] = value

        @pl.when(z != home)
        def _():
            arrival(out_ref, x2r).wait_recv()

        for k in range(1, pieces_n):
            x_copy(k).wait_send()
        for k in range(1, ny):
            y_copy(k).wait_send()
            y2_copy(k).wait_send()
        own_copy(0).wait_send()
        own_copy(1).wait_send()
        c_copy.wait_send()

        @pl.when(reducer)
        def _():
            for k in range(1, nz):
                t_copy(k).wait_send()

        def drain(i, carry):
            odd, dist, zb = offset(i)
            core_copy(zb).wait_send()
            go, copy = forward(i)

            @pl.when(go)
            def _():
                copy.wait_send()

            @pl.when(role_of(zb) != 0)
            def _():
                for h in range(2):
                    relay_copy(zb, h).wait_send()

            return carry

        lax.fori_loop(0, nz, drain, 0)

        @pl.when(z != home)
        def _():
            z2_copy.wait_send()

        @pl.when(z == home)
        def _():
            for k in range(1, pieces_n):
                x2_copy(k).wait_send()

    f32, bf16, i16 = jnp.float32, jnp.bfloat16, jnp.int16
    dma = pltpu.SemaphoreType.DMA
    scratch = [
        pltpu.VMEM((2 * depth, vocab), bf16),
        pltpu.VMEM((pieces_n, 8, depth + 128), f32),
        pltpu.VMEM((pieces_n, 8, depth + 128), f32),
        pltpu.VMEM((small, depth + 128), f32),
        pltpu.VMEM((ny, small, depth + 128), bf16),
        pltpu.VMEM((block, depth + 128), f32),
        pltpu.VMEM((nc, nz, block, depth), bf16),
        pltpu.VMEM((nz, 2, half, padded), f32),
        pltpu.VMEM((nz, 2, half, padded), i16),
        pltpu.VMEM((nz, half, padded), i16),
        pltpu.VMEM((nb, 2, 2, half, padded), i16),
        pltpu.VMEM((STAT, 128), f32),
        pltpu.VMEM((nb, 8, STAT), f32),
        pltpu.VMEM((nb, 8, STAT), f32),
        pltpu.VMEM((8, STAT), f32),
        pltpu.VMEM((ny, 8, STAT), f32),
        pltpu.VMEM((nz, 8, STAT), f32),
        pltpu.VMEM((8, STAT), f32),
        dma, dma((pieces_n,)), dma((pieces_n,)), dma((ny,)), dma((ny,)),
        dma((nz + 1,)), dma((nz,)), dma((nz,)), dma((nz,)), dma((nz,)), dma((nb,)),
        dma((nz, 2)), dma((nz,)), dma((nb, 2, 2)),
        dma, dma, dma((ny,)), dma((ny,)), dma, dma((nz,)), dma((pieces_n,)), dma,
    ]
    return kernel, scratch


def body(prefill_hidden, decode_hidden, lm_head, prefill_targets, decode_targets, decode_live):
    nx, nz = lax.axis_size("dp"), lax.axis_size("z")
    ny, nc = lax.axis_size("y"), lax.axis_size("c")
    pre, dec = prefill_hidden.shape[0], decode_hidden.shape[0]
    rows = pre + dec
    width, vocab = lm_head.shape
    kernel, scratch = make_kernel(nx, nz, ny, nc, rows, width // nc, vocab)
    vmem = pl.BlockSpec(memory_space=pltpu.VMEM)
    smem = pl.BlockSpec(memory_space=pltpu.SMEM)
    values = pl.pallas_call(
        kernel,
        out_shape=jax.ShapeDtypeStruct((8, STAT), jnp.float32),
        in_specs=[vmem, vmem, smem, smem, pl.BlockSpec(memory_space=pl.ANY)],
        out_specs=vmem,
        scratch_shapes=scratch,
        compiler_params=pltpu.CompilerParams(
            collective_id=0, has_side_effects=True, vmem_limit_bytes=60 << 20),
    )(prefill_hidden, decode_hidden, prefill_targets, decode_targets, lm_head)
    x, y, c = lax.axis_index("dp"), lax.axis_index("y"), lax.axis_index("c")
    at = (y * (nx * nc) + x * nc + c) * rows
    own = lax.dynamic_slice_in_dim(values[0], at, rows, 0)
    positions = lax.axis_index(VOCAB) * dec + jnp.arange(dec, dtype=jnp.int32)
    decode = jnp.where(positions < decode_live[0], own[pre:], jnp.float32(0.0))
    return own[:pre], decode


def solution(mesh):
    split = Mesh(mesh.devices.reshape(mesh.shape["dp"], 8, 4, 2), DP_VOCAB)
    placed = (
        P(DP_VOCAB, None),
        P(DP_VOCAB, None),
        P("dp", VOCAB),
        P(DP_VOCAB),
        P(DP_VOCAB),
        P("dp"),
    )
    return jax.shard_map(
        body, mesh=split, in_specs=placed, out_specs=(P(DP_VOCAB), P(DP_VOCAB)), check_vma=False
    )
```

time: 331 us -> 118 us (0.36)
  waiting for transfers between devices: 166 us -> 0 us
  blocking collectives: 110 us -> 0 us
  Pallas kernels: 0 us -> 99.8 us
  between operations: 17.9 us -> 3.72 us
  matrix products: 12.4 us -> 0 us
  other arithmetic: 6.4 us -> 0 us
    pallas_call x0 -> x1, Pallas kernels: none -> 99.8 us  [body(): pl.pallas_call(kernel, out_shape=jax.ShapeDtypeStruct((8, STAT), jnp.floa...]
    all_gather x1 -> x0, waiting for transfers between devices: 87 us -> none  [body(): lax.all_gather(hidden, VOCAB, axis=0, tiled=True)]
    reduce_scatter x1 -> x0, waiting for transfers between devices: 79.1 us -> none  [body(): lax.psum_scatter(jnp.dot(every_rows, lm_head, preferred_element_type=jnp....]
    all_to_all x1 -> x0, blocking collectives: 54.2 us -> none  [body(): lax.all_to_all(group_hidden, 'dp', split_axis=1, concat_axis=0, tiled=True)]
    all_gather x3 -> x0, blocking collectives: 40.8 us -> none  [gathered_once(): both, at, found = (lax.all_gather(jnp.concatenate(lines), axis), 0, {})]
    unnamed x1 -> x0, blocking collectives: 14.9 us -> none
    all_to_all x2 -> x0, local copies, waits for them, and re-layouts: 14.5 us -> none  [body(): lax.all_to_all(group_hidden, 'dp', split_axis=1, concat_axis=0, tiled=True)]
    dot_general x1 -> x0, matrix products: 12.4 us -> none  [body(): jnp.dot(every_rows, lm_head, preferred_element_type=jnp.float32)]
  transfers between devices with their start and end apart: 2 -> 0, of which waited for: 2 -> 0; matrix products, arithmetic and copies ran while one was open for 0% -> 0% of each run, Pallas kernels for 0% -> 0%
where the time goes in v1:
time: 118 us; the launch traced here: 116 us
  Pallas kernels  99.8 us (85%)
  local copies, waits for them, and re-layouts  12.4 us (11%)
  between operations  3.72 us (3%)
    pallas_call x1, Pallas kernels, body(): pl.pallas_call(kernel, out_shape=jax.ShapeDtypeStruct((8, STAT), jnp.floa...  99.8 us
    unnamed x1, local copies, waits for them, and re-layouts  10.5 us

profile of v1, /device:TPU:5, one launch (start us, length us, event | category | flops | bytes accessed | tf_op | source)
XLA Modules:
  0.0 115.9 jit_solution(8744096255360020963)
XLA Ops:
  1.3 10.5 %copy.8.w_hbm = bf16[1792,2020]{1,0:T(8,128)(2,1)} copy(bf16[1792,2020]{0,1:T(8,128)(2,1)} %param.8) | data formatting | bytes 14479360 | tf_op args[2]
  11.8 99.8 %shard_map.77 = f32[8,256]{1,0:T(8,128)} custom-call(bf16[4,7168]{1,0:T(4,128)(2,1)} %pre_ref.1, bf16[1,7168]{1,0:T(2,128)(2,1)} %dec_ref.1, s32[4]{0:T(128)} %pt_ref.1, s32[1]{0:T(128)S(6)} %copy.9.dt_ref, bf16[1792,2020]{1,0:T(8,128)(2,1)} %copy.8.w_hbm), custom_call_target="tpu_custom_call" | custom-call | tf_op jit(solution)/shard_map/pallas_call | solution.py:432
  111.6 0.7 slice.15
  112.3 0.1 constant_dynamic-slice_fusion
  112.4 0.5 slice_bitcast_fusion
  113.6 0.6 slice.18

commit v2 on v0

v2 whole, which is shorter than its diff:
```python
import jax
import jax.numpy as jnp
from jax import lax
from jax.experimental import pallas as pl
from jax.experimental.pallas import tpu as pltpu
from jax.sharding import Mesh
from jax.sharding import PartitionSpec as P

VOCAB = ("z", "y", "c")
DP_VOCAB = ("dp", "z", "y", "c")
MESH = pl.DeviceIdType.MESH
LANES = 128
CHUNK = 256
TOP = 32000.0


def make_kernel(nx, nz, ny, nc, rows, depth, vocab):
    pieces_n = nx * nc
    small = pieces_n * rows
    block = ny * small
    first_n = vocab // 32 * 16
    counts = (first_n, vocab - first_n)
    width = -(-(max(counts) + 1) // 512) * 512
    plane = nz * ny * nc

    def kernel(pre_ref, dec_ref, pt_ref, dt_ref, w_hbm, out_ref,
               w, pieces, xrecv, f40, ybuf, fblk, hall, part, sbuf, rel, rd,
               stat, tt, st, fin, res,
               w_sem, xs, xr, ys, yr, yf, yfr, ags, agr, d2s, d2r, ts, tr, rs, rlr, rdr,
               fs, fr, x2s, x2r):
        x = lax.axis_index("dp")
        z = lax.axis_index("z")
        y = lax.axis_index("y")
        c = lax.axis_index("c")
        other = 1 - c
        me = x * nc + c
        right = (lax.rem(x + 1, nx), z, y, c)
        left = (lax.rem(x + nx - 1, nx), z, y, c)
        w_copy = pltpu.make_async_copy(w_hbm, w, w_sem)
        w_copy.start()

        def send(src, dst, ssem, rsem, dev):
            return pltpu.make_async_remote_copy(
                src_ref=src, dst_ref=dst, send_sem=ssem, recv_sem=rsem,
                device_id=dev, device_id_type=MESH)

        def arrival(dst, sem):
            return send(dst, dst, sem, sem, (x, z, y, other))

        barrier = pltpu.get_barrier_semaphore()
        peers = []
        for k in range(1, pieces_n):
            p = lax.rem(me + k, pieces_n)
            peers.append((lax.div(p, nc), z, y, lax.rem(p, nc)))
        for k in range(1, ny):
            peers.append((x, z, lax.rem(y + k, ny), c))
        for k in (1, nz - 1):
            peers.append((x, lax.rem(z + k, nz), y, c))
        for dev in peers:
            pl.semaphore_signal(barrier, inc=1, device_id=dev, device_id_type=MESH)

        n_pre = pre_ref.shape[0]
        lane = lax.broadcasted_iota(jnp.int32, (rows, LANES), 1)
        row = lax.broadcasted_iota(jnp.int32, (rows, LANES), 0)
        ids = jnp.zeros((rows, LANES), jnp.int32)
        for r in range(rows):
            ids = jnp.where(row == r, pt_ref[r] if r < n_pre else dt_ref[r - n_pre], ids)
        digits = jnp.where(lane == 0, ids % 256,
                           jnp.where(lane == 1, (ids // 256) % 256,
                                     jnp.where(lane == 2, ids // 65536, 0))).astype(jnp.float32)
        for p in range(pieces_n):
            cols = slice(p * depth, (p + 1) * depth)
            own = jnp.concatenate([pre_ref[:, cols].astype(jnp.float32),
                                   dec_ref[:, cols].astype(jnp.float32)], axis=0)
            pieces[p, :, 0:depth] = own.astype(jnp.bfloat16)
            pieces[p, :, depth:depth + LANES] = digits.astype(jnp.bfloat16)
        for k in range(nz):
            for h in range(2):
                part[k, h, :, width - LANES:width] = jnp.zeros((block, LANES), jnp.float32)
        stat[...] = jnp.zeros(stat.shape, jnp.float32)

        pl.semaphore_wait(barrier, len(peers))

        def x_copy(k):
            p = lax.rem(me + k, pieces_n)
            return send(pieces.at[p], xrecv.at[me], xs.at[p], xr.at[me],
                        (lax.div(p, nc), z, y, lax.rem(p, nc)))

        for k in range(1, pieces_n):
            x_copy(k).start()
        xrecv[me] = pieces[me]
        for k in range(1, pieces_n):
            p = lax.rem(me + k, pieces_n)
            arrival(xrecv.at[p], xr.at[p]).wait_recv()
        for s in range(pieces_n):
            f40[s * rows:(s + 1) * rows, :] = xrecv[s].astype(jnp.float32)

        ybuf[y] = f40[...].astype(jnp.bfloat16)
        up, down = lax.rem(y + 1, ny), lax.rem(y + ny - 1, ny)
        mid = (depth + LANES) // 2

        def y_copy(way):
            return send(ybuf.at[y], ybuf.at[y], ys.at[way], yr.at[way],
                        (x, z, up if way else down, c))

        def y_forward(way):
            src = ybuf.at[down if way else up, :, pl.ds(way * mid, mid)]
            return send(src, src, yf.at[way], yfr.at[way], (x, z, up if way else down, c))

        y_copy(0).start()
        y_copy(1).start()
        for way in (1, 0):
            arrival(ybuf.at[down if way else up], yr.at[way]).wait_recv()
            y_forward(way).start()
        far = lax.rem(y + 2, ny)
        for way in (1, 0):
            arrival(ybuf.at[far, :, pl.ds(way * mid, mid)], yfr.at[way]).wait_recv()
        for s in range(ny):
            fblk[s * small:(s + 1) * small, :] = ybuf[s].astype(jnp.float32)
        hall[c, z] = fblk[:, 0:depth].astype(jnp.bfloat16)

        def own_copy(way):
            zz = lax.rem(z + (1 if way else nz - 1), nz)
            return send(hall.at[c, z], hall.at[c, z], ags.at[nz if way else z], agr.at[z],
                        (x, zz, y, c))

        def core_copy(zb):
            return send(hall.at[c, zb], hall.at[c, zb], d2s.at[zb], d2r.at[zb], (x, z, y, other))

        own_copy(0).start()
        own_copy(1).start()
        core_copy(z).start()

        digit = lax.broadcasted_iota(jnp.int32, (small, LANES), 1)
        weight = jnp.where(digit == 0, 1.0, jnp.where(digit == 1, 256.0,
                                                      jnp.where(digit == 2, 65536.0, 0.0)))
        at_x = pl.ds(pl.multiple_of(x * small, 8), small)
        named = jnp.sum(fblk[at_x, depth:depth + LANES] * weight, axis=1, keepdims=True)
        stat[0:small, :] = jnp.broadcast_to(named, (small, LANES))
        tt[z] = jnp.transpose(stat[...])[0:8, :]

        w_copy.wait()

        def block_of(i):
            odd = lax.rem(i, 2)
            dist = lax.div(i + 1, 2)
            return lax.rem(z + nz + jnp.where(odd == 1, dist, -dist), nz)

        def forward(dist, way):
            zb = lax.rem(z + nz + (-dist if way else dist), nz)
            zz = lax.rem(z + (1 if way else nz - 1), nz)
            return send(hall.at[c, zb], hall.at[c, zb], ags.at[zb], agr.at[zb], (x, zz, y, c))

        def product(rows_of, columns_of):
            return lax.dot_general(rows_of, columns_of, (((1,), (1,)), ((), ())),
                                   preferred_element_type=jnp.float32)

        def multiply(blocks):
            for h in range(2):
                base = h * first_n
                for n0 in range(0, counts[h], 512):
                    n1 = min(n0 + 512, counts[h])
                    at = slice(base + n0, base + n1)
                    lhs = [jnp.concatenate([hall[k, zb] for zb in blocks], axis=0)
                           if len(blocks) > 1 else hall[k, blocks[0]] for k in range(2)]
                    acc = product(lhs[0], w[at, 0:depth]) + product(lhs[1], w[at, depth:2 * depth])
                    for j, zb in enumerate(blocks):
                        part[zb, h, :, n0:n1] = acc[j * block:(j + 1) * block]

        def rows_at(q):
            return pl.ds(pl.multiple_of(q * small, 8), small)

        def step_of(code, h):
            return jnp.exp2(code[:, LANES - 1:LANES].astype(jnp.int32).astype(jnp.float32))

        def unpack(code, n0, h, step):
            v = code.astype(jnp.int32).astype(jnp.float32) * step
            if n0 + CHUNK > counts[h]:
                col = lax.broadcasted_iota(jnp.int32, v.shape, 1)
                v = jnp.where(col >= counts[h] - n0, 0.0, v)
            return v

        def quantise(zb, h, q, slot, relayed):
            at = rows_at(q)
            big = jnp.zeros((small, LANES), jnp.float32)
            if relayed:
                step = step_of(rel[zb, h, :, width - LANES:width], h)
            for n0 in range(0, width, CHUNK):
                v = part[zb, h, at, n0:n0 + CHUNK]
                if relayed:
                    v = v + unpack(rel[zb, h, :, n0:n0 + CHUNK], n0, h, step)
                    part[zb, h, at, n0:n0 + CHUNK] = v
                for k in range(0, CHUNK, LANES):
                    big = jnp.maximum(big, jnp.abs(v[:, k:k + LANES]))
            big = jnp.max(big, axis=1, keepdims=True)
            e = jnp.ceil(jnp.log2(jnp.maximum(big, 1e-20) * (1.0 / TOP)))
            scale = jnp.exp2(-e)
            for n0 in range(0, width, CHUNK):
                v = jnp.round(part[zb, h, at, n0:n0 + CHUNK] * scale)
                if n0 + CHUNK > counts[h]:
                    col = lax.broadcasted_iota(jnp.int32, v.shape, 1)
                    v = jnp.where(col >= counts[h] - n0, e, v)
                sbuf[zb, slot, :, n0:n0 + CHUNK] = v.astype(jnp.int32).astype(jnp.int16)

        toward_left = lax.rem(x + nx - 1, nx)
        toward_right = lax.rem(x + 1, nx)
        opposite = lax.rem(x + 2, nx)

        def message(zb, slot):
            if slot == 0:
                dst, rsem, dev = rel.at[zb, 0], rlr.at[zb, 0], left
            elif slot == 1:
                dst, rsem, dev = rel.at[zb, 1], rlr.at[zb, 1], right
            elif slot in (2, 4):
                h = 1 if slot == 2 else 0
                dst, rsem, dev = rd.at[zb, 0, h], rdr.at[zb, 0, h], left
            else:
                h = 0 if slot == 3 else 1
                dst, rsem, dev = rd.at[zb, 1, h], rdr.at[zb, 1, h], right
            return send(sbuf.at[zb, slot], dst, rs.at[zb, slot], rsem, dev)

        def emit(zb):
            for slot, h, q in ((0, 0, opposite), (1, 1, opposite),
                               (2, 1, toward_left), (3, 0, toward_right)):
                quantise(zb, h, q, slot, False)
                message(zb, slot).start()

        arrival(hall.at[other, z], d2r.at[z]).wait_recv()
        multiply([z])
        emit(z)

        def pair(dist, carry):
            above = lax.rem(z + dist, nz)
            below = lax.rem(z + nz - dist, nz)
            arrival(hall.at[c, above], agr.at[above]).wait_recv()
            core_copy(above).start()
            forward(dist, 0).start()
            arrival(hall.at[c, below], agr.at[below]).wait_recv()
            core_copy(below).start()

            @pl.when(dist < nz // 2 - 1)
            def _():
                forward(dist, 1).start()

            arrival(hall.at[other, above], d2r.at[above]).wait_recv()
            arrival(hall.at[other, below], d2r.at[below]).wait_recv()
            multiply([above, below])

            def one(j, carry):
                emit(jnp.where(j == 0, above, below))
                return carry

            lax.fori_loop(0, 2, one, 0)
            return carry

        lax.fori_loop(1, nz // 2, pair, 0)
        across = lax.rem(z + nz // 2, nz)
        arrival(hall.at[c, across], agr.at[across]).wait_recv()
        core_copy(across).start()
        arrival(hall.at[other, across], d2r.at[across]).wait_recv()
        multiply([across])
        emit(across)

        def t_copy(k):
            zz = lax.rem(z + k, nz)
            return send(tt.at[z], tt.at[z], ts.at[zz], tr.at[z], (x, zz, y, c))

        for k in range(1, nz):
            t_copy(k).start()

        def pass_on(i, carry):
            zb = block_of(i)
            arrival(rel.at[zb, 0], rlr.at[zb, 0]).wait_recv()
            quantise(zb, 0, toward_left, 4, True)
            message(zb, 4).start()
            arrival(rel.at[zb, 1], rlr.at[zb, 1]).wait_recv()
            quantise(zb, 1, toward_right, 5, True)
            message(zb, 5).start()
            return carry

        lax.fori_loop(0, nz, pass_on, 0)
        for k in range(1, nz):
            zz = lax.rem(z + k, nz)
            arrival(tt.at[zz], tr.at[zz]).wait_recv()

        first = (((z * ny + y) * nc + c) * vocab).astype(jnp.float32)
        mine = (z * ny + y) * nc + c
        at_row = rows_at(x)

        def home_of(zb):
            return (x, zb, x, lax.div(zb * nc, nz))

        def f_copy(zb):
            return send(st.at[zb], fin.at[mine], fs.at[zb], fr, home_of(zb))

        def is_home(zb):
            return jnp.logical_and(jnp.logical_and(z == zb, y == x), c == lax.div(zb * nc, nz))

        def reduce(i, carry):
            zb = block_of(i)
            wanted = jnp.transpose(jnp.broadcast_to(tt[zb, 0:1, :], (LANES, LANES)))[0:small, 0:1]
            big = jnp.full((small, LANES), -jnp.inf, jnp.float32)
            picked = jnp.zeros((small, LANES), jnp.float32)
            for h in range(2):
                for side in range(2):
                    arrival(rd.at[zb, side, h], rdr.at[zb, side, h]).wait_recv()
                steps = [step_of(rd[zb, side, h, :, width - LANES:width], h) for side in range(2)]
                local = (wanted - (first + float(h * first_n))).astype(jnp.int32)
                local = jnp.where(jnp.logical_and(local >= 0, local < counts[h]), local, -1)
                for n0 in range(0, width, CHUNK):
                    at = slice(n0, n0 + CHUNK)
                    v = part[zb, h, at_row, at] + (unpack(rd[zb, 0, h, :, at], n0, h, steps[0])
                                                   + unpack(rd[zb, 1, h, :, at], n0, h, steps[1]))
                    col = lax.broadcasted_iota(jnp.int32, v.shape, 1)
                    hit = jnp.where(col == local - n0, v, 0.0)
                    if n0 + CHUNK > counts[h]:
                        v = jnp.where(col >= counts[h] - n0, -jnp.inf, v)
                    part[zb, h, at_row, at] = v
                    for k in range(0, CHUNK, LANES):
                        big = jnp.maximum(big, v[:, k:k + LANES])
                        picked = picked + hit[:, k:k + LANES]
            top = jnp.max(big, axis=1, keepdims=True)
            total = jnp.zeros((small, LANES), jnp.float32)
            for h in range(2):
                for n0 in range(0, width, CHUNK):
                    v = jnp.exp(part[zb, h, at_row, n0:n0 + CHUNK] - top)
                    for k in range(0, CHUNK, LANES):
                        total = total + v[:, k:k + LANES]
            total = jnp.sum(total, axis=1, keepdims=True)
            picked = jnp.sum(picked, axis=1, keepdims=True)
            ln = lax.broadcasted_iota(jnp.int32, (small, LANES), 1)
            stat[0:small, :] = jnp.where(ln == 0, top, jnp.where(ln == 1, total,
                                                                jnp.where(ln == 2, picked, 0.0)))
            tile = jnp.transpose(stat[...])[0:3, :]
            st[zb] = tile

            @pl.when(is_home(zb))
            def _():
                fin[mine] = tile

            @pl.when(jnp.logical_not(is_home(zb)))
            def _():
                f_copy(zb).start()

            return carry

        lax.fori_loop(0, nz, reduce, 0)

        home = is_home(z)

        def x2_copy(k):
            p = lax.rem(me + k, pieces_n)
            return send(res, out_ref, x2s.at[p], x2r, (lax.div(p, nc), z, y, lax.rem(p, nc)))

        @pl.when(home)
        def _():
            arrival(fin.at[0:plane - 1], fr).wait_recv()
            tops = fin[:, 0, :]
            top = jnp.max(tops, axis=0, keepdims=True)
            total = jnp.sum(fin[:, 1, :] * jnp.exp(tops - top), axis=0, keepdims=True)
            picked = jnp.sum(fin[:, 2, :], axis=0, keepdims=True)
            value = jnp.broadcast_to(picked - (top + jnp.log(total)), (8, LANES))
            res[...] = value
            for k in range(1, pieces_n):
                x2_copy(k).start()
            out_ref[...] = value

        @pl.when(jnp.logical_not(home))
        def _():
            arrival(out_ref, x2r).wait_recv()

        for k in range(1, pieces_n):
            x_copy(k).wait_send()
        for way in range(2):
            y_copy(way).wait_send()
            y_forward(way).wait_send()
            own_copy(way).wait_send()
        for k in range(1, nz):
            t_copy(k).wait_send()

        def drain(i, carry):
            zb = block_of(i)
            core_copy(zb).wait_send()
            for slot in range(6):
                message(zb, slot).wait_send()

            @pl.when(jnp.logical_not(is_home(zb)))
            def _():
                f_copy(zb).wait_send()

            return carry

        lax.fori_loop(0, nz, drain, 0)
        for dist in range(1, nz // 2):
            forward(dist, 0).wait_send()
            if dist < nz // 2 - 1:
                forward(dist, 1).wait_send()

        @pl.when(home)
        def _():
            for k in range(1, pieces_n):
                x2_copy(k).wait_send()

    f32, bf16, i16 = jnp.float32, jnp.bfloat16, jnp.int16
    dma = pltpu.SemaphoreType.DMA
    scratch = [
        pltpu.VMEM((vocab, 2 * depth), bf16),
        pltpu.VMEM((pieces_n, rows, depth + LANES), bf16),
        pltpu.VMEM((pieces_n, rows, depth + LANES), bf16),
        pltpu.VMEM((small, depth + LANES), f32),
        pltpu.VMEM((ny, small, depth + LANES), bf16),
        pltpu.VMEM((block, depth + LANES), f32),
        pltpu.VMEM((nc, nz, block, depth), bf16),
        pltpu.VMEM((nz, 2, block, width), f32),
        pltpu.VMEM((nz, 6, small, width), i16),
        pltpu.VMEM((nz, 2, small, width), i16),
        pltpu.VMEM((nz, 2, 2, small, width), i16),
        pltpu.VMEM((LANES, LANES), f32),
        pltpu.VMEM((nz, 8, LANES), f32),
        pltpu.VMEM((nz, 3, LANES), f32),
        pltpu.VMEM((plane, 3, LANES), f32),
        pltpu.VMEM((8, LANES), f32),
        dma, dma((pieces_n,)), dma((pieces_n,)), dma((2,)), dma((2,)), dma((2,)), dma((2,)),
        dma((nz + 1,)), dma((nz,)), dma((nz,)), dma((nz,)), dma((nz,)), dma((nz,)),
        dma((nz, 6)), dma((nz, 2)), dma((nz, 2, 2)),
        dma((nz,)), dma, dma((pieces_n,)), dma,
    ]
    return kernel, scratch


def body(prefill_hidden, decode_hidden, lm_head, prefill_targets, decode_targets, decode_live):
    nx, nz = lax.axis_size("dp"), lax.axis_size("z")
    ny, nc = lax.axis_size("y"), lax.axis_size("c")
    pre, dec = prefill_hidden.shape[0], decode_hidden.shape[0]
    rows = pre + dec
    width, vocab = lm_head.shape
    kernel, scratch = make_kernel(nx, nz, ny, nc, rows, width // nc, vocab)
    vmem = pl.BlockSpec(memory_space=pltpu.VMEM)
    smem = pl.BlockSpec(memory_space=pltpu.SMEM)
    values = pl.pallas_call(
        kernel,
        out_shape=jax.ShapeDtypeStruct((8, LANES), jnp.float32),
        in_specs=[vmem, vmem, smem, smem, pl.BlockSpec(memory_space=pl.ANY)],
        out_specs=vmem,
        scratch_shapes=scratch,
        compiler_params=pltpu.CompilerParams(
            collective_id=0, has_side_effects=True, vmem_limit_bytes=60 << 20),
    )(prefill_hidden, decode_hidden, prefill_targets, decode_targets, lm_head.T)
    at = (lax.axis_index("dp") * nc + lax.axis_index("c")) * rows
    own = lax.dynamic_slice_in_dim(values[0], at, rows, 0)
    positions = lax.axis_index(VOCAB) * dec + jnp.arange(dec, dtype=jnp.int32)
    decode = jnp.where(positions < decode_live[0], own[pre:], jnp.float32(0.0))
    return own[:pre], decode


def solution(mesh):
    split = Mesh(mesh.devices.reshape(mesh.shape["dp"], 8, 4, 2), DP_VOCAB)
    placed = (
        P(DP_VOCAB, None),
        P(DP_VOCAB, None),
        P("dp", VOCAB),
        P(DP_VOCAB),
        P(DP_VOCAB),
        P("dp"),
    )
    return jax.shard_map(
        body, mesh=split, in_specs=placed, out_specs=(P(DP_VOCAB), P(DP_VOCAB)), check_vma=False
    )
```

time: 331 us -> 90.8 us (0.27)
  waiting for transfers between devices: 166 us -> 0 us
  blocking collectives: 110 us -> 0 us
  Pallas kernels: 0 us -> 85 us
  between operations: 17.9 us -> 3.72 us
  local copies, waits for them, and re-layouts: 15.7 us -> 1.85 us
  matrix products: 12.4 us -> 0 us
  other arithmetic: 6.4 us -> 0 us
    all_gather x1 -> x0, waiting for transfers between devices: 87 us -> none  [body(): lax.all_gather(hidden, VOCAB, axis=0, tiled=True)]
    pallas_call x0 -> x1, Pallas kernels: none -> 85 us  [body(): pl.pallas_call(kernel, out_shape=jax.ShapeDtypeStruct((8, LANES), jnp.flo...]
    reduce_scatter x1 -> x0, waiting for transfers between devices: 79.1 us -> none  [body(): lax.psum_scatter(jnp.dot(every_rows, lm_head, preferred_element_type=jnp....]
    all_to_all x1 -> x0, blocking collectives: 54.2 us -> none  [body(): lax.all_to_all(group_hidden, 'dp', split_axis=1, concat_axis=0, tiled=True)]
    all_gather x3 -> x0, blocking collectives: 40.8 us -> none  [gathered_once(): both, at, found = (lax.all_gather(jnp.concatenate(lines), axis), 0, {})]
    unnamed x1 -> x0, blocking collectives: 14.9 us -> none
    all_to_all x2 -> x0, local copies, waits for them, and re-layouts: 14.5 us -> none  [body(): lax.all_to_all(group_hidden, 'dp', split_axis=1, concat_axis=0, tiled=True)]
    dot_general x1 -> x0, matrix products: 12.4 us -> none  [body(): jnp.dot(every_rows, lm_head, preferred_element_type=jnp.float32)]
  transfers between devices with their start and end apart: 2 -> 0, of which waited for: 2 -> 0; matrix products, arithmetic and copies ran while one was open for 0% -> 0% of each run, Pallas kernels for 0% -> 0%
where the time goes in v2:
time: 90.8 us; the launch traced here: 90.6 us
  Pallas kernels  85 us (94%)
  between operations  3.72 us (4%)
  local copies, waits for them, and re-layouts  1.85 us (2%)
    pallas_call x1, Pallas kernels, body(): pl.pallas_call(kernel, out_shape=jax.ShapeDtypeStruct((8, LANES), jnp.flo...  85 us

profile of v2, /device:TPU:5, one launch (start us, length us, event | category | flops | bytes accessed | tf_op | source)
XLA Modules:
  0.0 90.6 jit_solution(16132090507255750763)
XLA Ops:
  1.3 85.0 %shard_map.77 = f32[8,128]{1,0:T(8,128)} custom-call(bf16[4,7168]{1,0:T(4,128)(2,1)} %pre_ref.1, bf16[1,7168]{1,0:T(2,128)(2,1)} %dec_ref.1, s32[4]{0:T(128)} %pt_ref.1, s32[1]{0:T(128)S(6)} %copy.8.dt_ref, bf16[2020,1792]{1,0:T(8,128)(2,1)} %bitcast.5), custom_call_target="tpu_custom_call" | custom-call | tf_op jit(solution)/shard_map/pallas_call | solution.py:440
  86.3 0.7 slice.15
  87.0 0.1 constant_dynamic-slice_fusion
  87.1 0.5 slice_bitcast_fusion
  88.2 0.6 slice.18

commit v3 on v2

--- a/solution.py
+++ b/solution.py
@@ -14,7 +14,7 @@
 TOP = 32000.0
 
 
-def make_kernel(nx, nz, ny, nc, rows, depth, vocab):
+def make_kernel(nx, nz, ny, nc, rows, n_dec, depth, vocab):
     pieces_n = nx * nc
     small = pieces_n * rows
     block = ny * small
@@ -23,10 +23,10 @@
     width = -(-(max(counts) + 1) // 512) * 512
     plane = nz * ny * nc
 
-    def kernel(pre_ref, dec_ref, pt_ref, dt_ref, w_hbm, out_ref,
-               w, pieces, xrecv, f40, ybuf, fblk, hall, part, sbuf, rel, rd,
-               stat, tt, st, fin, res,
-               w_sem, xs, xr, ys, yr, yf, yfr, ags, agr, d2s, d2r, ts, tr, rs, rlr, rdr,
+    def kernel(pre_hbm, dec_hbm, pt_hbm, dt_hbm, live_hbm, w_hbm, pre_hbm_out, dec_hbm_out,
+               pre_ref, dec_ref, pt_ref, dt_ref, live_ref, w, pieces, xrecv, f40, ybuf, fblk, hall, part, sbuf, rel, rd,
+               stat, tt, st, fin, res, got, pre_out, dec_out,
+               w_sem, in_sem, xs, xr, ys, yr, yf, yfr, ags, agr, d2s, d2r, ts, tr, rs, rlr, rdr,
                fs, fr, x2s, x2r):
         x = lax.axis_index("dp")
         z = lax.axis_index("z")
@@ -38,6 +38,11 @@
         left = (lax.rem(x + nx - 1, nx), z, y, c)
         w_copy = pltpu.make_async_copy(w_hbm, w, w_sem)
         w_copy.start()
+        inputs = [pltpu.make_async_copy(src, dst, in_sem.at[k]) for k, (src, dst) in enumerate(
+            ((pre_hbm, pre_ref), (dec_hbm, dec_ref), (pt_hbm, pt_ref), (dt_hbm, dt_ref),
+             (live_hbm, live_ref)))]
+        for copy in inputs:
+            copy.start()
 
         def send(src, dst, ssem, rsem, dev):
             return pltpu.make_async_remote_copy(
@@ -60,6 +65,8 @@
             pl.semaphore_signal(barrier, inc=1, device_id=dev, device_id_type=MESH)
 
         n_pre = pre_ref.shape[0]
+        for copy in inputs:
+            copy.wait()
         lane = lax.broadcasted_iota(jnp.int32, (rows, LANES), 1)
         row = lax.broadcasted_iota(jnp.int32, (rows, LANES), 0)
         ids = jnp.zeros((rows, LANES), jnp.int32)
@@ -99,22 +106,28 @@
         up, down = lax.rem(y + 1, ny), lax.rem(y + ny - 1, ny)
         mid = (depth + LANES) // 2
 
-        def y_copy(way):
-            return send(ybuf.at[y], ybuf.at[y], ys.at[way], yr.at[way],
+        def y_part(slot, k):
+            return ybuf.at[slot, :, pl.ds(k * mid, mid)]
+
+        def y_copy(way, k):
+            return send(y_part(y, k), y_part(y, k), ys.at[way, k], yr.at[way, k],
                         (x, z, up if way else down, c))
 
         def y_forward(way):
-            src = ybuf.at[down if way else up, :, pl.ds(way * mid, mid)]
+            src = y_part(down if way else up, way)
             return send(src, src, yf.at[way], yfr.at[way], (x, z, up if way else down, c))
 
-        y_copy(0).start()
-        y_copy(1).start()
+        for far_half in (True, False):
+            for way in (1, 0):
+                y_copy(way, way if far_half else 1 - way).start()
         for way in (1, 0):
-            arrival(ybuf.at[down if way else up], yr.at[way]).wait_recv()
+            arrival(y_part(down if way else up, way), yr.at[way, way]).wait_recv()
             y_forward(way).start()
         far = lax.rem(y + 2, ny)
         for way in (1, 0):
-            arrival(ybuf.at[far, :, pl.ds(way * mid, mid)], yfr.at[way]).wait_recv()
+            arrival(y_part(down if way else up, 1 - way), yr.at[way, 1 - way]).wait_recv()
+        for way in (1, 0):
+            arrival(y_part(far, way), yfr.at[way]).wait_recv()
         for s in range(ny):
             fblk[s * small:(s + 1) * small, :] = ybuf[s].astype(jnp.float32)
         hall[c, z] = fblk[:, 0:depth].astype(jnp.bfloat16)
@@ -139,6 +152,10 @@
         stat[0:small, :] = jnp.broadcast_to(named, (small, LANES))
         tt[z] = jnp.transpose(stat[...])[0:8, :]
 
+        def t_copy(k):
+            zz = lax.rem(z + k, nz)
+            return send(tt.at[z], tt.at[z], ts.at[zz], tr.at[z], (x, zz, y, c))
+
         w_copy.wait()
 
         def block_of(i):
@@ -155,17 +172,16 @@
             return lax.dot_general(rows_of, columns_of, (((1,), (1,)), ((), ())),
                                    preferred_element_type=jnp.float32)
 
-        def multiply(blocks):
-            for h in range(2):
-                base = h * first_n
-                for n0 in range(0, counts[h], 512):
-                    n1 = min(n0 + 512, counts[h])
-                    at = slice(base + n0, base + n1)
-                    lhs = [jnp.concatenate([hall[k, zb] for zb in blocks], axis=0)
-                           if len(blocks) > 1 else hall[k, blocks[0]] for k in range(2)]
-                    acc = product(lhs[0], w[at, 0:depth]) + product(lhs[1], w[at, depth:2 * depth])
-                    for j, zb in enumerate(blocks):
-                        part[zb, h, :, n0:n1] = acc[j * block:(j + 1) * block]
+        def multiply(blocks, h):
+            base = h * first_n
+            for n0 in range(0, counts[h], 512):
+                n1 = min(n0 + 512, counts[h])
+                at = slice(base + n0, base + n1)
+                lhs = [jnp.concatenate([hall[k, zb] for zb in blocks], axis=0)
+                       if len(blocks) > 1 else hall[k, blocks[0]] for k in range(2)]
+                acc = product(lhs[0], w[at, 0:depth]) + product(lhs[1], w[at, depth:2 * depth])
+                for j, zb in enumerate(blocks):
+                    part[zb, h, :, n0:n1] = acc[j * block:(j + 1) * block]
 
         def rows_at(q):
             return pl.ds(pl.multiple_of(q * small, 8), small)
@@ -219,15 +235,30 @@
                 dst, rsem, dev = rd.at[zb, 1, h], rdr.at[zb, 1, h], right
             return send(sbuf.at[zb, slot], dst, rs.at[zb, slot], rsem, dev)
 
-        def emit(zb):
-            for slot, h, q in ((0, 0, opposite), (1, 1, opposite),
-                               (2, 1, toward_left), (3, 0, toward_right)):
-                quantise(zb, h, q, slot, False)
+        def emit(zb, h, slots):
+            for slot in slots:
+                quantise(zb, h, {2: toward_left, 3: toward_right}.get(slot, opposite), slot, False)
                 message(zb, slot).start()
 
+        def pass_on(zb):
+            arrival(rel.at[zb, 0], rlr.at[zb, 0]).wait_recv()
+            quantise(zb, 0, toward_left, 4, True)
+            message(zb, 4).start()
+            arrival(rel.at[zb, 1], rlr.at[zb, 1]).wait_recv()
+            quantise(zb, 1, toward_right, 5, True)
+            message(zb, 5).start()
+
+        def pass_pair(dist):
+            def one(j, carry):
+                pass_on(lax.rem(z + nz + jnp.where(j == 0, dist, -dist), nz))
+                return carry
+
+            lax.fori_loop(0, 2, one, 0)
+
         arrival(hall.at[other, z], d2r.at[z]).wait_recv()
-        multiply([z])
-        emit(z)
+        for h in range(2):
+            multiply([z], h)
+            emit(z, h, (h, 3 - h))
 
         def pair(dist, carry):
             above = lax.rem(z + dist, nz)
@@ -242,46 +273,42 @@
             def _():
                 forward(dist, 1).start()
 
+            t_copy(dist).start()
+            t_copy(nz - dist).start()
+
+            @pl.when(dist == 1)
+            def _():
+                pass_on(z)
+
             arrival(hall.at[other, above], d2r.at[above]).wait_recv()
             arrival(hall.at[other, below], d2r.at[below]).wait_recv()
-            multiply([above, below])
-
-            def one(j, carry):
-                emit(jnp.where(j == 0, above, below))
-                return carry
-
-            lax.fori_loop(0, 2, one, 0)
+            for h in range(2):
+                multiply([above, below], h)
+
+                def one(j, carry):
+                    emit(jnp.where(j == 0, above, below), h, (h, 3 - h))
+                    return carry
+
+                lax.fori_loop(0, 2, one, 0)
+                if h == 0:
+                    @pl.when(dist > 1)
+                    def _():
+                        pass_pair(dist - 1)
+
             return carry
 
         lax.fori_loop(1, nz // 2, pair, 0)
         across = lax.rem(z + nz // 2, nz)
         arrival(hall.at[c, across], agr.at[across]).wait_recv()
         core_copy(across).start()
+        t_copy(nz // 2).start()
         arrival(hall.at[other, across], d2r.at[across]).wait_recv()
-        multiply([across])
-        emit(across)
-
-        def t_copy(k):
-            zz = lax.rem(z + k, nz)
-            return send(tt.at[z], tt.at[z], ts.at[zz], tr.at[z], (x, zz, y, c))
-
-        for k in range(1, nz):
-            t_copy(k).start()
-
-        def pass_on(i, carry):
-            zb = block_of(i)
-            arrival(rel.at[zb, 0], rlr.at[zb, 0]).wait_recv()
-            quantise(zb, 0, toward_left, 4, True)
-            message(zb, 4).start()
-            arrival(rel.at[zb, 1], rlr.at[zb, 1]).wait_recv()
-            quantise(zb, 1, toward_right, 5, True)
-            message(zb, 5).start()
-            return carry
-
-        lax.fori_loop(0, nz, pass_on, 0)
-        for k in range(1, nz):
-            zz = lax.rem(z + k, nz)
-            arrival(tt.at[zz], tr.at[zz]).wait_recv()
+        for h in range(2):
+            multiply([across], h)
+            emit(across, h, (h,))
+        pass_pair(nz // 2 - 1)
+        for h in range(2):
+            emit(across, h, (3 - h,))
 
         first = (((z * ny + y) * nc + c) * vocab).astype(jnp.float32)
         mine = (z * ny + y) * nc + c
@@ -298,6 +325,11 @@
 
         def reduce(i, carry):
             zb = block_of(i)
+
+            @pl.when(zb != z)
+            def _():
+                arrival(tt.at[zb], tr.at[zb]).wait_recv()
+
             wanted = jnp.transpose(jnp.broadcast_to(tt[zb, 0:1, :], (LANES, LANES)))[0:small, 0:1]
             big = jnp.full((small, LANES), -jnp.inf, jnp.float32)
             picked = jnp.zeros((small, LANES), jnp.float32)
@@ -344,13 +376,43 @@
 
             return carry
 
-        lax.fori_loop(0, nz, reduce, 0)
+        early = nz - 3
+        lax.fori_loop(0, early, reduce, 0)
+        pass_on(across)
+        lax.fori_loop(early, nz, reduce, 0)
+        for k in range(1, pieces_n):
+            x_copy(k).wait_send()
+        for way in range(2):
+            for k in range(2):
+                y_copy(way, k).wait_send()
+            y_forward(way).wait_send()
+            own_copy(way).wait_send()
+        for k in range(1, nz):
+            t_copy(k).wait_send()
+
+        def drain(i, carry):
+            zb = block_of(i)
+            core_copy(zb).wait_send()
+            for slot in range(6):
+                message(zb, slot).wait_send()
+
+            @pl.when(jnp.logical_not(is_home(zb)))
+            def _():
+                f_copy(zb).wait_send()
+
+            return carry
+
+        lax.fori_loop(0, nz, drain, 0)
+        for dist in range(1, nz // 2):
+            forward(dist, 0).wait_send()
+            if dist < nz // 2 - 1:
+                forward(dist, 1).wait_send()
 
         home = is_home(z)
 
         def x2_copy(k):
             p = lax.rem(me + k, pieces_n)
-            return send(res, out_ref, x2s.at[p], x2r, (lax.div(p, nc), z, y, lax.rem(p, nc)))
+            return send(res, got, x2s.at[p], x2r, (lax.div(p, nc), z, y, lax.rem(p, nc)))
 
         @pl.when(home)
         def _():
@@ -363,47 +425,39 @@
             res[...] = value
             for k in range(1, pieces_n):
                 x2_copy(k).start()
-            out_ref[...] = value
+            got[...] = value
 
         @pl.when(jnp.logical_not(home))
         def _():
-            arrival(out_ref, x2r).wait_recv()
-
-        for k in range(1, pieces_n):
-            x_copy(k).wait_send()
-        for way in range(2):
-            y_copy(way).wait_send()
-            y_forward(way).wait_send()
-            own_copy(way).wait_send()
-        for k in range(1, nz):
-            t_copy(k).wait_send()
-
-        def drain(i, carry):
-            zb = block_of(i)
-            core_copy(zb).wait_send()
-            for slot in range(6):
-                message(zb, slot).wait_send()
-
-            @pl.when(jnp.logical_not(is_home(zb)))
-            def _():
-                f_copy(zb).wait_send()
-
-            return carry
-
-        lax.fori_loop(0, nz, drain, 0)
-        for dist in range(1, nz // 2):
-            forward(dist, 0).wait_send()
-            if dist < nz // 2 - 1:
-                forward(dist, 1).wait_send()
+            arrival(got, x2r).wait_recv()
+
+        values = pltpu.roll(got[...], LANES - me * rows, 1)
+        lanes = lax.broadcasted_iota(jnp.int32, (8, LANES), 1)
+        position = mine * n_dec + lanes - n_pre
+        values = jnp.where(jnp.logical_and(lanes >= n_pre, position >= live_ref[0]), 0.0, values)
+        pre_out[...] = values[0, 0:n_pre]
+        dec_out[...] = values[0, n_pre:rows]
+        outputs = [pltpu.make_async_copy(pre_out, pre_hbm_out, in_sem.at[0]),
+                   pltpu.make_async_copy(dec_out, dec_hbm_out, in_sem.at[1])]
+        for copy in outputs:
+            copy.start()
 
         @pl.when(home)
         def _():
             for k in range(1, pieces_n):
                 x2_copy(k).wait_send()
 
+        for copy in outputs:
+            copy.wait()
+
     f32, bf16, i16 = jnp.float32, jnp.bfloat16, jnp.int16
     dma = pltpu.SemaphoreType.DMA
     scratch = [
+        pltpu.VMEM((rows - n_dec, nx * nc * depth), bf16),
+        pltpu.VMEM((n_dec, nx * nc * depth), bf16),
+        pltpu.SMEM((rows - n_dec,), jnp.int32),
+        pltpu.SMEM((n_dec,), jnp.int32),
+        pltpu.SMEM((1,), jnp.int32),
         pltpu.VMEM((vocab, 2 * depth), bf16),
         pltpu.VMEM((pieces_n, rows, depth + LANES), bf16),
         pltpu.VMEM((pieces_n, rows, depth + LANES), bf16),
@@ -420,7 +474,10 @@
         pltpu.VMEM((nz, 3, LANES), f32),
         pltpu.VMEM((plane, 3, LANES), f32),
         pltpu.VMEM((8, LANES), f32),
-        dma, dma((pieces_n,)), dma((pieces_n,)), dma((2,)), dma((2,)), dma((2,)), dma((2,)),
+        pltpu.VMEM((8, LANES), f32),
+        pltpu.VMEM((rows - n_dec,), f32),
+        pltpu.VMEM((n_dec,), f32),
+        dma, dma((5,)), dma((pieces_n,)), dma((pieces_n,)), dma((2, 2)), dma((2, 2)), dma((2,)), dma((2,)),
         dma((nz + 1,)), dma((nz,)), dma((nz,)), dma((nz,)), dma((nz,)), dma((nz,)),
         dma((nz, 6)), dma((nz, 2)), dma((nz, 2, 2)),
         dma((nz,)), dma, dma((pieces_n,)), dma,
@@ -434,23 +491,18 @@
     pre, dec = prefill_hidden.shape[0], decode_hidden.shape[0]
     rows = pre + dec
     width, vocab = lm_head.shape
-    kernel, scratch = make_kernel(nx, nz, ny, nc, rows, width // nc, vocab)
-    vmem = pl.BlockSpec(memory_space=pltpu.VMEM)
-    smem = pl.BlockSpec(memory_space=pltpu.SMEM)
-    values = pl.pallas_call(
+    kernel, scratch = make_kernel(nx, nz, ny, nc, rows, dec, width // nc, vocab)
+    hbm = pl.BlockSpec(memory_space=pltpu.HBM)
+    return pl.pallas_call(
         kernel,
-        out_shape=jax.ShapeDtypeStruct((8, LANES), jnp.float32),
-        in_specs=[vmem, vmem, smem, smem, pl.BlockSpec(memory_space=pl.ANY)],
-        out_specs=vmem,
+        out_shape=(jax.ShapeDtypeStruct((pre,), jnp.float32),
+                   jax.ShapeDtypeStruct((dec,), jnp.float32)),
+        in_specs=[hbm] * 6,
+        out_specs=(hbm, hbm),
         scratch_shapes=scratch,
         compiler_params=pltpu.CompilerParams(
             collective_id=0, has_side_effects=True, vmem_limit_bytes=60 << 20),
-    )(prefill_hidden, decode_hidden, prefill_targets, decode_targets, lm_head.T)
-    at = (lax.axis_index("dp") * nc + lax.axis_index("c")) * rows
-    own = lax.dynamic_slice_in_dim(values[0], at, rows, 0)
-    positions = lax.axis_index(VOCAB) * dec + jnp.arange(dec, dtype=jnp.int32)
-    decode = jnp.where(positions < decode_live[0], own[pre:], jnp.float32(0.0))
-    return own[:pre], decode
+    )(prefill_hidden, decode_hidden, prefill_targets, decode_targets, decode_live, lm_head.T)
 
 
 def solution(mesh):

time: 90.8 us -> 85.4 us (0.941)
  Pallas kernels: 85 us -> 80.4 us
    pallas_call x1, Pallas kernels: 85 us -> 80.4 us  [body(): pl.pallas_call(kernel, out_shape=(jax.ShapeDtypeStruct((pre,), jnp.float3...]
    slice x3 -> x0, local copies, waits for them, and re-layouts: 1.78 us -> none  [the longest x1 0.68 us: body(): own = lax.dynamic_slice_in_dim(values[0], at, rows, 0)]
    unnamed x0 -> x1, local copies, waits for them, and re-layouts: none -> 1.11 us
where the time goes in v3:
time: 85.4 us; the launch traced here: 85.2 us
  Pallas kernels  80.4 us (94%)
  between operations  3.69 us (4%)
  local copies, waits for them, and re-layouts  1.11 us (1%)
    pallas_call x1, Pallas kernels, body(): pl.pallas_call(kernel, out_shape=(jax.ShapeDtypeStruct((pre,), jnp.float3...  80.4 us

profile of v3, /device:TPU:5, one launch (start us, length us, event | category | flops | bytes accessed | tf_op | source)
XLA Modules:
  0.0 85.2 jit_solution(613178081105407770)
XLA Ops:
  1.9 80.4 %shard_map.77 = (f32[4]{0:T(128)}, f32[1]{0:T(128)}) custom-call(bf16[4,7168]{1,0:T(4,128)(2,1)} %pre_hbm.1, bf16[1,7168]{1,0:T(2,128)(2,1)} %dec_hbm.1, s32[4]{0:T(128)} %pt_hbm.1, s32[1]{0:T(128)S(6)} %copy.10.dt_hbm, s32[1]{0:T(128)S(6)} %copy.11.live_hbm, bf16[2020,1792]{1,0:T(8,128)(2,1)} %bitcast.1), custom_call_target="tpu_custom_call" | custom-call | tf_op jit(solution)/shard_map/pallas_call | solution.py:496
  82.4 1.1 %copy.12 = f32[4]{0:T(128)} copy(f32[4]{0:T(128)} %get-tuple-element.4) | data formatting | bytes 32

commit v4 on v3

--- a/solution.py
+++ b/solution.py
@@ -24,7 +24,7 @@
     plane = nz * ny * nc
 
     def kernel(pre_hbm, dec_hbm, pt_hbm, dt_hbm, live_hbm, w_hbm, pre_hbm_out, dec_hbm_out,
-               pre_ref, dec_ref, pt_ref, dt_ref, live_ref, w, pieces, xrecv, f40, ybuf, fblk, hall, part, sbuf, rel, rd,
+               pre_ref, dec_ref, pt_ref, dt_ref, live_ref, w, pieces, xrecv, f40, ybuf, hall, dense, part, sbuf, rel, rd,
                stat, tt, st, fin, res, got, pre_out, dec_out,
                w_sem, in_sem, xs, xr, ys, yr, yf, yfr, ags, agr, d2s, d2r, ts, tr, rs, rlr, rdr,
                fs, fr, x2s, x2r):
@@ -34,8 +34,8 @@
         c = lax.axis_index("c")
         other = 1 - c
         me = x * nc + c
-        right = (lax.rem(x + 1, nx), z, y, c)
-        left = (lax.rem(x + nx - 1, nx), z, y, c)
+        x_up = (lax.rem(x + 1, nx), z, y, c)
+        x_down = (lax.rem(x + nx - 1, nx), z, y, c)
         w_copy = pltpu.make_async_copy(w_hbm, w, w_sem)
         w_copy.start()
         inputs = [pltpu.make_async_copy(src, dst, in_sem.at[k]) for k, (src, dst) in enumerate(
@@ -90,15 +90,13 @@
 
         def x_copy(k):
             p = lax.rem(me + k, pieces_n)
-            return send(pieces.at[p], xrecv.at[me], xs.at[p], xr.at[me],
+            return send(pieces.at[p], xrecv.at[me], xs, xr,
                         (lax.div(p, nc), z, y, lax.rem(p, nc)))
 
         for k in range(1, pieces_n):
             x_copy(k).start()
         xrecv[me] = pieces[me]
-        for k in range(1, pieces_n):
-            p = lax.rem(me + k, pieces_n)
-            arrival(xrecv.at[p], xr.at[p]).wait_recv()
+        arrival(xrecv.at[0:pieces_n - 1], xr).wait_recv()
         for s in range(pieces_n):
             f40[s * rows:(s + 1) * rows, :] = xrecv[s].astype(jnp.float32)
 
@@ -110,51 +108,82 @@
             return ybuf.at[slot, :, pl.ds(k * mid, mid)]
 
         def y_copy(way, k):
-            return send(y_part(y, k), y_part(y, k), ys.at[way, k], yr.at[way, k],
+            return send(y_part(y, k), y_part(y, k), ys, yr.at[way, k],
                         (x, z, up if way else down, c))
 
         def y_forward(way):
             src = y_part(down if way else up, way)
-            return send(src, src, yf.at[way], yfr.at[way], (x, z, up if way else down, c))
+            return send(src, src, yf, yfr.at[way], (x, z, up if way else down, c))
+
+        above_z, below_z = lax.rem(z + 1, nz), lax.rem(z + nz - 1, nz)
+
+        def spread(j):
+            src = ybuf.at[j, :, pl.ds(0, depth)]
+            for zz in (above_z, below_z):
+                send(src, hall.at[c, z, j], ags, agr.at[z, j], (x, zz, y, c)).start()
+            send(src, hall.at[c, z, j], d2s, d2r.at[z], (x, z, y, other)).start()
+            hall[c, z, j] = ybuf[j, :, 0:depth]
+
+        def take(dist, parts):
+            up_zb, down_zb = lax.rem(z + dist, nz), lax.rem(z + nz - dist, nz)
+
+            def ring(zb, j, zz):
+                return send(hall.at[c, zb, j], hall.at[c, zb, j], ags, agr.at[zb, j],
+                            (x, zz, y, c))
+
+            def got_rows(zb, j):
+                arrival(hall.at[c, zb, j], agr.at[zb, j]).wait_recv()
+
+            def core_copy(zb, j):
+                return send(hall.at[c, zb, j], hall.at[c, zb, j], d2s, d2r.at[zb],
+                            (x, z, y, other))
+
+            for j in parts:
+                got_rows(up_zb, j)
+
+                @pl.when(dist < nz // 2)
+                def _():
+                    ring(up_zb, j, below_z).start()
+                    got_rows(down_zb, j)
+
+                @pl.when(dist < nz // 2 - 1)
+                def _():
+                    ring(down_zb, j, above_z).start()
+
+                core_copy(up_zb, j).start()
+
+                @pl.when(dist < nz // 2)
+                def _():
+                    core_copy(down_zb, j).start()
 
         for far_half in (True, False):
             for way in (1, 0):
                 y_copy(way, way if far_half else 1 - way).start()
+        spread(y)
         for way in (1, 0):
             arrival(y_part(down if way else up, way), yr.at[way, way]).wait_recv()
             y_forward(way).start()
+        for way in (1, 0):
+            arrival(y_part(down if way else up, 1 - way), yr.at[way, 1 - way]).wait_recv()
+            spread(down if way else up)
         far = lax.rem(y + 2, ny)
         for way in (1, 0):
-            arrival(y_part(down if way else up, 1 - way), yr.at[way, 1 - way]).wait_recv()
-        for way in (1, 0):
             arrival(y_part(far, way), yfr.at[way]).wait_recv()
-        for s in range(ny):
-            fblk[s * small:(s + 1) * small, :] = ybuf[s].astype(jnp.float32)
-        hall[c, z] = fblk[:, 0:depth].astype(jnp.bfloat16)
-
-        def own_copy(way):
-            zz = lax.rem(z + (1 if way else nz - 1), nz)
-            return send(hall.at[c, z], hall.at[c, z], ags.at[nz if way else z], agr.at[z],
-                        (x, zz, y, c))
-
-        def core_copy(zb):
-            return send(hall.at[c, zb], hall.at[c, zb], d2s.at[zb], d2r.at[zb], (x, z, y, other))
-
-        own_copy(0).start()
-        own_copy(1).start()
-        core_copy(z).start()
+        spread(far)
+        one_hop = z * 0 + 1
+        take(one_hop, (y,))
 
         digit = lax.broadcasted_iota(jnp.int32, (small, LANES), 1)
         weight = jnp.where(digit == 0, 1.0, jnp.where(digit == 1, 256.0,
                                                       jnp.where(digit == 2, 65536.0, 0.0)))
-        at_x = pl.ds(pl.multiple_of(x * small, 8), small)
-        named = jnp.sum(fblk[at_x, depth:depth + LANES] * weight, axis=1, keepdims=True)
+        mine_digits = ybuf[x, :, depth:depth + LANES].astype(jnp.float32)
+        named = jnp.sum(mine_digits * weight, axis=1, keepdims=True)
         stat[0:small, :] = jnp.broadcast_to(named, (small, LANES))
         tt[z] = jnp.transpose(stat[...])[0:8, :]
 
         def t_copy(k):
             zz = lax.rem(z + k, nz)
-            return send(tt.at[z], tt.at[z], ts.at[zz], tr.at[z], (x, zz, y, c))
+            return send(tt.at[z], tt.at[z], ts, tr, (x, zz, y, c))
 
         w_copy.wait()
 
@@ -163,23 +192,25 @@
             dist = lax.div(i + 1, 2)
             return lax.rem(z + nz + jnp.where(odd == 1, dist, -dist), nz)
 
-        def forward(dist, way):
-            zb = lax.rem(z + nz + (-dist if way else dist), nz)
-            zz = lax.rem(z + (1 if way else nz - 1), nz)
-            return send(hall.at[c, zb], hall.at[c, zb], ags.at[zb], agr.at[zb], (x, zz, y, c))
-
         def product(rows_of, columns_of):
             return lax.dot_general(rows_of, columns_of, (((1,), (1,)), ((), ())),
                                    preferred_element_type=jnp.float32)
 
+        def align(blocks):
+            for k in range(2):
+                for c0 in range(0, depth, LANES):
+                    rows_of = jnp.concatenate([hall[k, zb, j, :, c0:c0 + LANES].astype(jnp.float32)
+                                               for zb in blocks for j in range(ny)], axis=0)
+                    dense[k, 0:len(blocks) * block, c0:c0 + LANES] = rows_of.astype(jnp.bfloat16)
+
         def multiply(blocks, h):
             base = h * first_n
+            n_rows = len(blocks) * block
             for n0 in range(0, counts[h], 512):
                 n1 = min(n0 + 512, counts[h])
                 at = slice(base + n0, base + n1)
-                lhs = [jnp.concatenate([hall[k, zb] for zb in blocks], axis=0)
-                       if len(blocks) > 1 else hall[k, blocks[0]] for k in range(2)]
-                acc = product(lhs[0], w[at, 0:depth]) + product(lhs[1], w[at, depth:2 * depth])
+                acc = (product(dense[0, 0:n_rows], w[at, 0:depth])
+                       + product(dense[1, 0:n_rows], w[at, depth:2 * depth]))
                 for j, zb in enumerate(blocks):
                     part[zb, h, :, n0:n1] = acc[j * block:(j + 1) * block]
 
@@ -224,16 +255,16 @@
 
         def message(zb, slot):
             if slot == 0:
-                dst, rsem, dev = rel.at[zb, 0], rlr.at[zb, 0], left
+                dst, rsem, dev = rel.at[zb, 0], rlr.at[zb, 0], x_down
             elif slot == 1:
-                dst, rsem, dev = rel.at[zb, 1], rlr.at[zb, 1], right
+                dst, rsem, dev = rel.at[zb, 1], rlr.at[zb, 1], x_up
             elif slot in (2, 4):
                 h = 1 if slot == 2 else 0
-                dst, rsem, dev = rd.at[zb, 0, h], rdr.at[zb, 0, h], left
+                dst, rsem, dev = rd.at[zb, 0, h], rdr.at[zb], x_down
             else:
                 h = 0 if slot == 3 else 1
-                dst, rsem, dev = rd.at[zb, 1, h], rdr.at[zb, 1, h], right
-            return send(sbuf.at[zb, slot], dst, rs.at[zb, slot], rsem, dev)
+                dst, rsem, dev = rd.at[zb, 1, h], rdr.at[zb], x_up
+            return send(sbuf.at[zb, slot], dst, rs, rsem, dev)
 
         def emit(zb, h, slots):
             for slot in slots:
@@ -257,40 +288,42 @@
 
         arrival(hall.at[other, z], d2r.at[z]).wait_recv()
         for h in range(2):
+            if h == 0:
+                align([z])
             multiply([z], h)
             emit(z, h, (h, 3 - h))
+            take(one_hop, (up, down) if h == 0 else (far,))
 
         def pair(dist, carry):
             above = lax.rem(z + dist, nz)
             below = lax.rem(z + nz - dist, nz)
-            arrival(hall.at[c, above], agr.at[above]).wait_recv()
-            core_copy(above).start()
-            forward(dist, 0).start()
-            arrival(hall.at[c, below], agr.at[below]).wait_recv()
-            core_copy(below).start()
-
-            @pl.when(dist < nz // 2 - 1)
-            def _():
-                forward(dist, 1).start()
-
             t_copy(dist).start()
             t_copy(nz - dist).start()
-
-            @pl.when(dist == 1)
-            def _():
-                pass_on(z)
 
             arrival(hall.at[other, above], d2r.at[above]).wait_recv()
             arrival(hall.at[other, below], d2r.at[below]).wait_recv()
             for h in range(2):
+                if h == 0:
+                    align([above, below])
                 multiply([above, below], h)
 
                 def one(j, carry):
-                    emit(jnp.where(j == 0, above, below), h, (h, 3 - h))
+                    zb = jnp.where(j == 0, above, below)
+                    emit(zb, h, (h,))
+
+                    @pl.when(dist > 1)
+                    def _():
+                        emit(zb, h, (3 - h,))
+
                     return carry
 
                 lax.fori_loop(0, 2, one, 0)
+                take(dist + 1, (y, up) if h == 0 else (down, far))
                 if h == 0:
+                    @pl.when(dist == 1)
+                    def _():
+                        pass_on(z)
+
                     @pl.when(dist > 1)
                     def _():
                         pass_pair(dist - 1)
@@ -299,11 +332,11 @@
 
         lax.fori_loop(1, nz // 2, pair, 0)
         across = lax.rem(z + nz // 2, nz)
-        arrival(hall.at[c, across], agr.at[across]).wait_recv()
-        core_copy(across).start()
         t_copy(nz // 2).start()
         arrival(hall.at[other, across], d2r.at[across]).wait_recv()
         for h in range(2):
+            if h == 0:
+                align([across])
             multiply([across], h)
             emit(across, h, (h,))
         pass_pair(nz // 2 - 1)
@@ -318,24 +351,18 @@
             return (x, zb, x, lax.div(zb * nc, nz))
 
         def f_copy(zb):
-            return send(st.at[zb], fin.at[mine], fs.at[zb], fr, home_of(zb))
+            return send(st.at[zb], fin.at[mine], fs, fr, home_of(zb))
 
         def is_home(zb):
             return jnp.logical_and(jnp.logical_and(z == zb, y == x), c == lax.div(zb * nc, nz))
 
         def reduce(i, carry):
             zb = block_of(i)
-
-            @pl.when(zb != z)
-            def _():
-                arrival(tt.at[zb], tr.at[zb]).wait_recv()
-
+            arrival(rd.at[zb], rdr.at[zb]).wait_recv()
             wanted = jnp.transpose(jnp.broadcast_to(tt[zb, 0:1, :], (LANES, LANES)))[0:small, 0:1]
             big = jnp.full((small, LANES), -jnp.inf, jnp.float32)
             picked = jnp.zeros((small, LANES), jnp.float32)
             for h in range(2):
-                for side in range(2):
-                    arrival(rd.at[zb, side, h], rdr.at[zb, side, h]).wait_recv()
                 steps = [step_of(rd[zb, side, h, :, width - LANES:width], h) for side in range(2)]
                 local = (wanted - (first + float(h * first_n))).astype(jnp.int32)
                 local = jnp.where(jnp.logical_and(local >= 0, local < counts[h]), local, -1)
@@ -376,43 +403,43 @@
 
             return carry
 
-        early = nz - 3
-        lax.fori_loop(0, early, reduce, 0)
+        arrival(tt.at[0:nz - 1], tr).wait_recv()
+        reduce(0, 0)
+        lax.fori_loop(3, nz - 2, reduce, 0)
         pass_on(across)
-        lax.fori_loop(early, nz, reduce, 0)
-        for k in range(1, pieces_n):
-            x_copy(k).wait_send()
-        for way in range(2):
-            for k in range(2):
-                y_copy(way, k).wait_send()
-            y_forward(way).wait_send()
-            own_copy(way).wait_send()
-        for k in range(1, nz):
-            t_copy(k).wait_send()
-
-        def drain(i, carry):
-            zb = block_of(i)
-            core_copy(zb).wait_send()
-            for slot in range(6):
-                message(zb, slot).wait_send()
-
-            @pl.when(jnp.logical_not(is_home(zb)))
-            def _():
-                f_copy(zb).wait_send()
-
+
+        def near(j, carry):
+            zb = block_of(j)
+            for h in range(2):
+                emit(zb, h, (3 - h,))
             return carry
 
-        lax.fori_loop(0, nz, drain, 0)
-        for dist in range(1, nz // 2):
-            forward(dist, 0).wait_send()
-            if dist < nz // 2 - 1:
-                forward(dist, 1).wait_send()
+        lax.fori_loop(1, 3, near, 0)
+        lax.fori_loop(nz - 2, nz, reduce, 0)
+        lax.fori_loop(1, 3, reduce, 0)
+        def left(ref, sem):
+            send(ref, ref, sem, sem, (x, z, y, other)).wait_send()
 
         home = is_home(z)
+        left(pieces.at[0:pieces_n - 1], xs)
+        left(ybuf.at[0:2], ys)
+        left(ybuf.at[0], yf)
+        left(hall.at[c, 0:nz - 1], ags)
+        left(hall.at[c], d2s)
+        left(tt.at[0:nz - 1], ts)
+        left(sbuf, rs)
+
+        @pl.when(home)
+        def _():
+            left(st.at[0:nz - 1], fs)
+
+        @pl.when(jnp.logical_not(home))
+        def _():
+            left(st, fs)
 
         def x2_copy(k):
             p = lax.rem(me + k, pieces_n)
-            return send(res, got, x2s.at[p], x2r, (lax.div(p, nc), z, y, lax.rem(p, nc)))
+            return send(res, got, x2s, x2r, (lax.div(p, nc), z, y, lax.rem(p, nc)))
 
         @pl.when(home)
         def _():
@@ -444,8 +471,7 @@
 
         @pl.when(home)
         def _():
-            for k in range(1, pieces_n):
-                x2_copy(k).wait_send()
+            left(tt.at[0:pieces_n - 1], x2s)
 
         for copy in outputs:
             copy.wait()
@@ -463,8 +489,8 @@
         pltpu.VMEM((pieces_n, rows, depth + LANES), bf16),
         pltpu.VMEM((small, depth + LANES), f32),
         pltpu.VMEM((ny, small, depth + LANES), bf16),
-        pltpu.VMEM((block, depth + LANES), f32),
-        pltpu.VMEM((nc, nz, block, depth), bf16),
+        pltpu.VMEM((nc, nz, ny, small, depth), bf16),
+        pltpu.VMEM((2, 2 * block, depth), bf16),
         pltpu.VMEM((nz, 2, block, width), f32),
         pltpu.VMEM((nz, 6, small, width), i16),
         pltpu.VMEM((nz, 2, small, width), i16),
@@ -477,10 +503,10 @@
         pltpu.VMEM((8, LANES), f32),
         pltpu.VMEM((rows - n_dec,), f32),
         pltpu.VMEM((n_dec,), f32),
-        dma, dma((5,)), dma((pieces_n,)), dma((pieces_n,)), dma((2, 2)), dma((2, 2)), dma((2,)), dma((2,)),
-        dma((nz + 1,)), dma((nz,)), dma((nz,)), dma((nz,)), dma((nz,)), dma((nz,)),
-        dma((nz, 6)), dma((nz, 2)), dma((nz, 2, 2)),
-        dma((nz,)), dma, dma((pieces_n,)), dma,
+        dma, dma((5,)), dma, dma, dma, dma((2, 2)), dma, dma((2,)),
+        dma, dma((nz, ny)), dma, dma((nz,)), dma, dma,
+        dma, dma((nz, 2)), dma((nz,)),
+        dma, dma, dma, dma,
     ]
     return kernel, scratch
 

time: 85.4 us -> 82.1 us (0.961)
  Pallas kernels: 80.4 us -> 77.1 us
    pallas_call x1, Pallas kernels: 80.4 us -> 77.1 us  [body(): pl.pallas_call(kernel, out_shape=(jax.ShapeDtypeStruct((pre,), jnp.float3...]
where the time goes in v4:
time: 82.1 us; the launch traced here: 81.9 us
  Pallas kernels  77.1 us (94%)
  between operations  3.69 us (4%)
  local copies, waits for them, and re-layouts  1.11 us (1%)
    pallas_call x1, Pallas kernels, body(): pl.pallas_call(kernel, out_shape=(jax.ShapeDtypeStruct((pre,), jnp.float3...  77.1 us

profile of v4, /device:TPU:5, one launch (start us, length us, event | category | flops | bytes accessed | tf_op | source)
XLA Modules:
  0.0 81.9 jit_solution(10427111251978826716)
XLA Ops:
  1.9 77.1 %shard_map.77 = (f32[4]{0:T(128)}, f32[1]{0:T(128)}) custom-call(bf16[4,7168]{1,0:T(4,128)(2,1)} %pre_hbm.1, bf16[1,7168]{1,0:T(2,128)(2,1)} %dec_hbm.1, s32[4]{0:T(128)} %pt_hbm.1, s32[1]{0:T(128)S(6)} %copy.10.dt_hbm, s32[1]{0:T(128)S(6)} %copy.11.live_hbm, bf16[2020,1792]{1,0:T(8,128)(2,1)} %bitcast.1), custom_call_target="tpu_custom_call" | custom-call | tf_op jit(solution)/shard_map/pallas_call | solution.py:522
  79.1 1.1 %copy.12 = f32[4]{0:T(128)} copy(f32[4]{0:T(128)} %get-tuple-element.4) | data formatting | bytes 32

commit v5 on v4

--- a/solution.py
+++ b/solution.py
@@ -25,9 +25,9 @@
 
     def kernel(pre_hbm, dec_hbm, pt_hbm, dt_hbm, live_hbm, w_hbm, pre_hbm_out, dec_hbm_out,
                pre_ref, dec_ref, pt_ref, dt_ref, live_ref, w, pieces, xrecv, f40, ybuf, hall, dense, part, sbuf, rel, rd,
-               stat, tt, st, fin, res, got, pre_out, dec_out,
+               stat, tt, st, fin, pre_out, dec_out,
                w_sem, in_sem, xs, xr, ys, yr, yf, yfr, ags, agr, d2s, d2r, ts, tr, rs, rlr, rdr,
-               fs, fr, x2s, x2r):
+               fs, fr):
         x = lax.axis_index("dp")
         z = lax.axis_index("z")
         y = lax.axis_index("y")
@@ -347,14 +347,8 @@
         mine = (z * ny + y) * nc + c
         at_row = rows_at(x)
 
-        def home_of(zb):
-            return (x, zb, x, lax.div(zb * nc, nz))
-
-        def f_copy(zb):
-            return send(st.at[zb], fin.at[mine], fs, fr, home_of(zb))
-
-        def is_home(zb):
-            return jnp.logical_and(jnp.logical_and(z == zb, y == x), c == lax.div(zb * nc, nz))
+        def f_copy(zb, p):
+            return send(st.at[zb], fin.at[mine], fs, fr, (lax.div(p, nc), zb, x, lax.rem(p, nc)))
 
         def reduce(i, carry):
             zb = block_of(i)
@@ -390,17 +384,24 @@
             ln = lax.broadcasted_iota(jnp.int32, (small, LANES), 1)
             stat[0:small, :] = jnp.where(ln == 0, top, jnp.where(ln == 1, total,
                                                                 jnp.where(ln == 2, picked, 0.0)))
-            tile = jnp.transpose(stat[...])[0:3, :]
+            tile = jnp.transpose(stat[...])[0:8, :]
+            ln = lax.broadcasted_iota(jnp.int32, (1, LANES), 1)
+            tile = jnp.where(ln < small, tile[0:1, :],
+                             jnp.where(ln < 2 * small, pltpu.roll(tile, small, 1)[1:2, :],
+                                       pltpu.roll(tile, 2 * small, 1)[2:3, :]))
             st[zb] = tile
-
-            @pl.when(is_home(zb))
+            own_rows = jnp.logical_and(z == zb, y == x)
+
+            @pl.when(own_rows)
             def _():
                 fin[mine] = tile
 
-            @pl.when(jnp.logical_not(is_home(zb)))
+            @pl.when(jnp.logical_not(own_rows))
             def _():
-                f_copy(zb).start()
-
+                f_copy(zb, me).start()
+
+            for k in range(1, pieces_n):
+                f_copy(zb, lax.rem(me + k, pieces_n)).start()
             return carry
 
         arrival(tt.at[0:nz - 1], tr).wait_recv()
@@ -420,7 +421,7 @@
         def left(ref, sem):
             send(ref, ref, sem, sem, (x, z, y, other)).wait_send()
 
-        home = is_home(z)
+        owner = x == y
         left(pieces.at[0:pieces_n - 1], xs)
         left(ybuf.at[0:2], ys)
         left(ybuf.at[0], yf)
@@ -429,36 +430,23 @@
         left(tt.at[0:nz - 1], ts)
         left(sbuf, rs)
 
-        @pl.when(home)
+        @pl.when(owner)
         def _():
-            left(st.at[0:nz - 1], fs)
-
-        @pl.when(jnp.logical_not(home))
+            left(fin.at[0:plane - 1], fs)
+            arrival(fin.at[0:plane - 1], fr).wait_recv()
+
+        @pl.when(jnp.logical_not(owner))
         def _():
-            left(st, fs)
-
-        def x2_copy(k):
-            p = lax.rem(me + k, pieces_n)
-            return send(res, got, x2s, x2r, (lax.div(p, nc), z, y, lax.rem(p, nc)))
-
-        @pl.when(home)
-        def _():
-            arrival(fin.at[0:plane - 1], fr).wait_recv()
-            tops = fin[:, 0, :]
-            top = jnp.max(tops, axis=0, keepdims=True)
-            total = jnp.sum(fin[:, 1, :] * jnp.exp(tops - top), axis=0, keepdims=True)
-            picked = jnp.sum(fin[:, 2, :], axis=0, keepdims=True)
-            value = jnp.broadcast_to(picked - (top + jnp.log(total)), (8, LANES))
-            res[...] = value
-            for k in range(1, pieces_n):
-                x2_copy(k).start()
-            got[...] = value
-
-        @pl.when(jnp.logical_not(home))
-        def _():
-            arrival(got, x2r).wait_recv()
-
-        values = pltpu.roll(got[...], LANES - me * rows, 1)
+            left(fin, fs)
+            arrival(fin, fr).wait_recv()
+
+        tops = fin[:, 0, :]
+        top = jnp.max(tops, axis=0, keepdims=True)
+        weights = jnp.exp(tops - top)
+        total = jnp.sum(pltpu.roll(tops, LANES - small, 1) * weights, axis=0, keepdims=True)
+        picked = jnp.sum(pltpu.roll(tops, LANES - 2 * small, 1), axis=0, keepdims=True)
+        joined = jnp.broadcast_to(picked - (top + jnp.log(total)), (8, LANES))
+        values = pltpu.roll(joined, LANES - me * rows, 1)
         lanes = lax.broadcasted_iota(jnp.int32, (8, LANES), 1)
         position = mine * n_dec + lanes - n_pre
         values = jnp.where(jnp.logical_and(lanes >= n_pre, position >= live_ref[0]), 0.0, values)
@@ -468,10 +456,6 @@
                    pltpu.make_async_copy(dec_out, dec_hbm_out, in_sem.at[1])]
         for copy in outputs:
             copy.start()
-
-        @pl.when(home)
-        def _():
-            left(tt.at[0:pieces_n - 1], x2s)
 
         for copy in outputs:
             copy.wait()
@@ -497,16 +481,14 @@
         pltpu.VMEM((nz, 2, 2, small, width), i16),
         pltpu.VMEM((LANES, LANES), f32),
         pltpu.VMEM((nz, 8, LANES), f32),
-        pltpu.VMEM((nz, 3, LANES), f32),
-        pltpu.VMEM((plane, 3, LANES), f32),
-        pltpu.VMEM((8, LANES), f32),
-        pltpu.VMEM((8, LANES), f32),
+        pltpu.VMEM((nz, 1, LANES), f32),
+        pltpu.VMEM((plane, 1, LANES), f32),
         pltpu.VMEM((rows - n_dec,), f32),
         pltpu.VMEM((n_dec,), f32),
         dma, dma((5,)), dma, dma, dma, dma((2, 2)), dma, dma((2,)),
         dma, dma((nz, ny)), dma, dma((nz,)), dma, dma,
         dma, dma((nz, 2)), dma((nz,)),
-        dma, dma, dma, dma,
+        dma, dma,
     ]
     return kernel, scratch
 

time: 82.1 us -> 80.8 us (0.984); the launches traced: 81.9 us -> 79.8 us
  Pallas kernels: 77.1 us -> 75 us
    pallas_call x1, Pallas kernels: 77.1 us -> 75 us  [body(): pl.pallas_call(kernel, out_shape=(jax.ShapeDtypeStruct((pre,), jnp.float3...]
where the time goes in v5:
time: 80.8 us; the launch traced here: 79.8 us
  Pallas kernels  75 us (93%)
  between operations  3.69 us (5%)
  local copies, waits for them, and re-layouts  1.11 us (1%)
    pallas_call x1, Pallas kernels, body(): pl.pallas_call(kernel, out_shape=(jax.ShapeDtypeStruct((pre,), jnp.float3...  75 us

profile of v5, /device:TPU:5, one launch (start us, length us, event | category | flops | bytes accessed | tf_op | source)
XLA Modules:
  0.0 79.8 jit_solution(1892829659858362942)
XLA Ops:
  1.9 75.0 %shard_map.77 = (f32[4]{0:T(128)}, f32[1]{0:T(128)}) custom-call(bf16[4,7168]{1,0:T(4,128)(2,1)} %pre_hbm.1, bf16[1,7168]{1,0:T(2,128)(2,1)} %dec_hbm.1, s32[4]{0:T(128)} %pt_hbm.1, s32[1]{0:T(128)S(6)} %copy.10.dt_hbm, s32[1]{0:T(128)S(6)} %copy.11.live_hbm, bf16[2020,1792]{1,0:T(8,128)(2,1)} %bitcast.1), custom_call_target="tpu_custom_call" | custom-call | tf_op jit(solution)/shard_map/pallas_call | solution.py:504
  76.9 1.1 %copy.12 = f32[4]{0:T(128)} copy(f32[4]{0:T(128)} %get-tuple-element.4) | data formatting | bytes 32

commit v6 on v5

--- a/solution.py
+++ b/solution.py
@@ -311,7 +311,7 @@
                     zb = jnp.where(j == 0, above, below)
                     emit(zb, h, (h,))
 
-                    @pl.when(dist > 1)
+                    @pl.when(dist > j)
                     def _():
                         emit(zb, h, (3 - h,))
 
@@ -405,7 +405,7 @@
             return carry
 
         arrival(tt.at[0:nz - 1], tr).wait_recv()
-        reduce(0, 0)
+        lax.fori_loop(0, 2, reduce, 0)
         lax.fori_loop(3, nz - 2, reduce, 0)
         pass_on(across)
 
@@ -415,9 +415,9 @@
                 emit(zb, h, (3 - h,))
             return carry
 
-        lax.fori_loop(1, 3, near, 0)
+        near(2, 0)
         lax.fori_loop(nz - 2, nz, reduce, 0)
-        lax.fori_loop(1, 3, reduce, 0)
+        reduce(2, 0)
         def left(ref, sem):
             send(ref, ref, sem, sem, (x, z, y, other)).wait_send()
 

time: 80.8 us -> 80.9 us (level)
  no operation moved by 1% of the time
where the time goes in v6:
time: 80.9 us; the launch traced here: 79.9 us
  Pallas kernels  75.1 us (93%)
  between operations  3.69 us (5%)
  local copies, waits for them, and re-layouts  1.11 us (1%)
    pallas_call x1, Pallas kernels, body(): pl.pallas_call(kernel, out_shape=(jax.ShapeDtypeStruct((pre,), jnp.float3...  75.1 us

profile of v6, /device:TPU:5, one launch (start us, length us, event | category | flops | bytes accessed | tf_op | source)
XLA Modules:
  0.0 79.9 jit_solution(1222249653331843815)
XLA Ops:
  1.9 75.1 %shard_map.77 = (f32[4]{0:T(128)}, f32[1]{0:T(128)}) custom-call(bf16[4,7168]{1,0:T(4,128)(2,1)} %pre_hbm.1, bf16[1,7168]{1,0:T(2,128)(2,1)} %dec_hbm.1, s32[4]{0:T(128)} %pt_hbm.1, s32[1]{0:T(128)S(6)} %copy.10.dt_hbm, s32[1]{0:T(128)S(6)} %copy.11.live_hbm, bf16[2020,1792]{1,0:T(8,128)(2,1)} %bitcast.1), custom_call_target="tpu_custom_call" | custom-call | tf_op jit(solution)/shard_map/pallas_call | solution.py:504
  77.0 1.1 %copy.12 = f32[4]{0:T(128)} copy(f32[4]{0:T(128)} %get-tuple-element.4) | data formatting | bytes 32
